TPU v7x, 32 devices: a whole 2x2x4 slice. The times are simulated.
32 devices in a mesh: groups: 2 (over y), blk: 4 (over z), rep: 2 (over x), sub: 2 (over core).
Axes of the slice: x: 2, y: 2, z: 4, core: 2. Of those that a mesh axis runs over, the one named last changes fastest.
Arguments:
- replica_delta: bfloat16 [32, 32, 4608], P(('groups', 'blk', 'rep', 'sub')), parts along dimension 0, may hold values from -150 to 150
- momentum: float32 [64, 4608], P(('groups', 'blk')), parts along dimension 0, may hold values from -6 to 6
- params: float32 [64, 4608], P(('groups', 'blk')), parts along dimension 0, may hold values from -6 to 6
- prev_master: float32 [64, 4608], P(('groups', 'blk')), parts along dimension 0, may hold values from -6 to 6
Outputs:
- new_params: float32 [64, 4608], P(('groups', 'blk')), parts along dimension 0
- new_momentum: float32 [64, 4608], P(('groups', 'blk')), parts along dimension 0
- prev_weights: bfloat16 [64, 4608], P('groups'), parts along dimension 0
There are 2 independent parts, one for each index of `groups`. A program takes and returns all parts, laid end to end along the dimension named above; each array names one. Nothing has to cross between parts.
All inputs are finite; a program needn't handle non-finite values.
Results may differ from a plain program's by a relative error of at most 0.012.
Values may be sent and summed in bfloat16 or wider, within the bound.
No kernel may reach another device: no remote copies, remote signals or barrier semaphores. Data moves between devices by JAX's collectives and lax.ppermute only.
A program may use at most 64 MiB of HBM per device.

v0:
```python
import jax
import jax.numpy as jnp
from jax import lax
from jax.sharding import PartitionSpec as P

momentum_coef = 0.9
outer_rate = 0.7


def per_device(replica_delta, momentum, params, prev_master):
    own_delta = replica_delta[0]
    width = own_delta.shape[1]
    entries = own_delta.shape[0] * width
    share_sum = lax.psum_scatter(
        own_delta.astype(jnp.float32).astype(jnp.bfloat16), "blk", scatter_dimension=0, tiled=True
    )
    summed = lax.psum(share_sum, ("rep", "sub")).astype(jnp.float32)
    squares = lax.psum(jnp.sum(summed * summed), "blk")
    clip_factor = jnp.minimum(
        jnp.float32(1.0), jnp.sqrt(jnp.float32(entries)) / jnp.sqrt(squares + 1e-06)
    )
    scaled = clip_factor * summed
    new_momentum = momentum_coef * momentum + scaled
    new_params = params - outer_rate * (scaled + momentum_coef * new_momentum)
    prev_weights = lax.all_gather(prev_master.astype(jnp.bfloat16), "blk", axis=0, tiled=True)
    return (new_params, new_momentum, prev_weights)


def solution(mesh):
    in_specs = (
        P(("groups", "blk", "rep", "sub"), None, None),
        P(("groups", "blk"), None),
        P(("groups", "blk"), None),
        P(("groups", "blk"), None),
    )
    out_specs = (P(("groups", "blk"), None), P(("groups", "blk"), None), P("groups", None))
    return jax.shard_map(
        per_device, mesh=mesh, in_specs=in_specs, out_specs=out_specs, check_vma=False
    )
```

profile of v0, /device:TPU:0, one launch (start us, length us, event | category | flops | bytes accessed | tf_op | source)
XLA Modules:
  0.0 86.8 jit_solution(3447558341183904942)
XLA Ops:
  7.2 0.0 reduce-scatter.2.cloned.1.call-start
  7.2 0.0 copy-start.1
  7.2 0.7 reduce-scatter.2.cloned.1.call-update
  7.9 0.0 all-reduce.2.cloned.1.call-start
  7.9 0.2 copy-done.1
  8.1 25.1 %reduce-scatter.2.cloned.1.call-done = bf16[8,4608]{1,0:T(8,128)(2,1)} async-done(((bf16[32,4608]{1,0:T(8,128)(2,1)}), bf16[8,4608]{1,0:T(8,128)(2,1)}) %reduce-scatter.2.cloned.1.call-update) | async-done | bytes 73744 | tf_op jit(solution)/shard_map/reduce_scatter | solution.py:14
  33.2 0.0 all-reduce.2.cloned.1.call-update
  33.2 0.0 copy-start.2
  33.2 0.0 copy-start.3
  33.2 14.1 %all_gather.3 = bf16[32,4608]{1,0:T(8,128)(2,1)S(1)} all-gather(bf16[8,4608]{1,0:T(8,128)(2,1)S(1)} %convert_element_type.9), channel_id=1, replica_groups=mesh['groups'=2,'blk'=4,'rep'=2,'sub'=2] {'blk'}, dimensions={0}, use_global_device_ids=true | all-gather | bytes 368640 | tf_op jit(solution)/shard_map/all_gather | solution.py:25
  47.4 16.1 %all-reduce.2.cloned.1.call-done = bf16[8,4608]{1,0:T(8,128)(2,1)} async-done(((bf16[8,4608]{1,0:T(8,128)(2,1)}), bf16[8,4608]{1,0:T(8,128)(2,1)}) %all-reduce.2.cloned.1.call-update) | async-done | bytes 73744 | tf_op jit(solution)/shard_map/psum | solution.py:17
  63.5 0.0 copy-start
  63.5 1.6 %fusion.4 = f32[]{:T(128)} fusion(bf16[8,4608]{1,0:T(8,128)(2,1)} %all-reduce.2.cloned.1.call-done), kind=kLoop, calls=%fused_computation.6 | loop fusion | flops 110591 | bytes 73732 | tf_op jit(solution)/shard_map/reduce_sum | solution.py:18
  65.1 12.7 %psum.15 = f32[]{:T(128)} all-reduce(f32[]{:T(128)} %fusion.4), channel_id=1, replica_groups=mesh['groups'=2,'blk'=4,'rep'=2,'sub'=2] {'blk'}, use_global_device_ids=true, to_apply=%region_3.0 | all-reduce | flops 1 | bytes 8 | tf_op jit(solution)/shard_map/psum | solution.py:18
  78.4 0.0 copy-done.2
  78.5 0.0 copy-done.3
  78.5 0.0 copy-done
  78.5 0.8 fusion.3
  79.2 0.7 copy.9
  (1 shorter events, 0.0 us)
Async XLA Ops:
  7.2 26.0 %reduce-scatter.2.cloned.1.call-start = ((), (), s32[]{:S(2)}) async-start(), calls=%async_computation.1 | async-start | bytes 368640 | tf_op jit(solution)/shard_map/reduce_scatter | solution.py:14
  7.2 0.9 %copy-start.1 = (f32[8,4608]{1,0:T(8,128)S(1)}, f32[8,4608]{1,0:T(8,128)}, u32[]{:S(2)}) copy-start(f32[8,4608]{1,0:T(8,128)} %param.7) | copy-start | bytes 442372
  7.9 55.6 %all-reduce.2.cloned.1.call-start = ((), (), s32[]{:S(2)}) async-start(), calls=%async_computation.2 | async-start | bytes 147456 | tf_op jit(solution)/shard_map/psum | solution.py:17
  33.2 45.2 %copy-start.2 = (f32[8,4608]{1,0:T(8,128)S(1)}, f32[8,4608]{1,0:T(8,128)}, u32[]{:S(2)}) copy-start(f32[8,4608]{1,0:T(8,128)} %param.6) | copy-start | bytes 442372
  33.2 45.2 %copy-start.3 = (f32[8,4608]{1,0:T(8,128)S(1)}, f32[8,4608]{1,0:T(8,128)}, u32[]{:S(2)}) copy-start(f32[8,4608]{1,0:T(8,128)} %param.5) | copy-start | bytes 442372
  63.5 15.0 %copy-start = (bf16[8,4608]{1,0:T(8,128)(2,1)S(1)}, bf16[8,4608]{1,0:T(8,128)(2,1)}, u32[]{:S(2)}) copy-start(bf16[8,4608]{1,0:T(8,128)(2,1)} %all-reduce.2.cloned.1.call-done) | copy-start | bytes 221188
Sparse Core Ops, SparseCore 0:
  10.2 22.9 reduce-scatter.1
  35.5 27.9 all-reduce.1
where the time goes:
time: 87 us; the launch traced here: 86.8 us
  waiting for transfers between devices  41.9 us (48%)
  blocking collectives  26.8 us (31%)
  between operations  14.8 us (17%)
  other arithmetic  2.36 us (3%)
  local copies, waits for them, and re-layouts  0.91 us (1%)
    reduce_scatter x1, waiting for transfers between devices, per_device(): lax.psum_scatter(own_delta.astype(jnp.float32).astype(jnp.bfloat16), 'blk...  25.1 us
    psum x1, waiting for transfers between devices, per_device(): summed = lax.psum(share_sum, ('rep', 'sub')).astype(jnp.float32)  16.1 us
    all_gather x1, blocking collectives, per_device(): lax.all_gather(prev_master.astype(jnp.bfloat16), 'blk', axis=0, tiled=True)  14.1 us
    psum x1, blocking collectives, per_device(): squares = lax.psum(jnp.sum(summed * summed), 'blk')  12.7 us
  transfers between devices with their start and end apart: 2, of which 2 were waited for; matrix products, arithmetic and copies ran while one was open for 0% of the time, Pallas kernels for 0%

commit v1 on v0

v1 whole, which is shorter than its diff:
```python
import jax
import jax.numpy as jnp
from jax import lax
from jax.sharding import PartitionSpec as P

momentum_coef = 0.9
outer_rate = 0.7
F32 = jnp.float32
BF16 = jnp.bfloat16
BLK_DIRECT = False


def swap(value, axis, size, bit):
    return lax.ppermute(value, axis, [(i, i ^ bit) for i in range(size)])


def bits_of(size):
    return [1 << k for k in range(size.bit_length() - 1)]


def make(mesh):
    n_blk, n_rep, n_sub = mesh.shape["blk"], mesh.shape["rep"], mesh.shape["sub"]

    def halves(value, axis, size, bit):
        index = lax.axis_index(axis)
        half = value.shape[1] // 2
        mine = (index // bit) % 2
        keep = lax.dynamic_slice_in_dim(value, mine * half, half, 1)
        away = lax.dynamic_slice_in_dim(value, (1 - mine) * half, half, 1)
        return keep, away

    def joined(own, other, axis, bit, dim):
        upper = (lax.axis_index(axis) // bit) % 2 == 1
        return jnp.concatenate(
            [jnp.where(upper, other, own), jnp.where(upper, own, other)], axis=dim
        )

    def per_device(replica_delta, momentum, params, prev_master):
        delta = replica_delta[0]
        rows = momentum.shape[0]
        entries = delta.shape[0] * delta.shape[1]
        blk = lax.axis_index("blk")

        other = swap(delta, "sub", n_sub, 1)
        total = delta.astype(F32) + other.astype(F32)
        total, _ = halves(total, "sub", n_sub, 1)
        for bit in reversed(bits_of(n_rep)):
            keep, away = halves(total, "rep", n_rep, bit)
            total = keep + swap(away.astype(BF16), "rep", n_rep, bit).astype(F32)
        if BLK_DIRECT:
            sent = total.astype(BF16)
            for k in range(1, n_blk):
                total = total + swap(sent, "blk", n_blk, k).astype(F32)
        else:
            for bit in bits_of(n_blk):
                total = total + swap(total.astype(BF16), "blk", n_blk, bit).astype(F32)
        squares = jnp.sum(total * total)
        own = lax.dynamic_slice_in_dim(total, blk * rows, rows, 0)

        for axis, size in (("rep", n_rep), ("sub", n_sub)):
            for bit in bits_of(size):
                packed = jnp.concatenate([own, jnp.full((rows, 128), squares, F32)], axis=1)
                got = swap(packed, axis, size, bit)
                width = own.shape[1]
                own = joined(own, got[:, :width], axis, bit, 1)
                squares = squares + got[0, width]

        clip_factor = jnp.minimum(
            jnp.float32(1.0), jnp.sqrt(jnp.float32(entries)) / jnp.sqrt(squares + 1e-06)
        )
        scaled = clip_factor * own
        new_momentum = momentum_coef * momentum + scaled
        new_params = params - outer_rate * (scaled + momentum_coef * new_momentum)

        prev = prev_master.astype(BF16)
        prev, _ = halves(prev, "sub", n_sub, 1)
        for bit in reversed(bits_of(n_rep)):
            prev, _ = halves(prev, "rep", n_rep, bit)
        for bit in bits_of(n_blk):
            prev = joined(prev, swap(prev, "blk", n_blk, bit), "blk", bit, 0)
        for axis, size in (("rep", n_rep), ("sub", n_sub)):
            for bit in bits_of(size):
                prev = joined(prev, swap(prev, axis, size, bit), axis, bit, 1)
        return (new_params, new_momentum, prev)

    return per_device


def solution(mesh):
    in_specs = (
        P(("groups", "blk", "rep", "sub"), None, None),
        P(("groups", "blk"), None),
        P(("groups", "blk"), None),
        P(("groups", "blk"), None),
    )
    out_specs = (P(("groups", "blk"), None), P(("groups", "blk"), None), P("groups", None))
    return jax.shard_map(
        make(mesh), mesh=mesh, in_specs=in_specs, out_specs=out_specs, check_vma=False
    )
```

time: 87 us -> 39.5 us (0.45)
  blocking collectives: 26.8 us -> 0 us
  waiting for transfers between devices: 41.9 us -> 15.7 us
  starting transfers between devices: 0.08 us -> 13.6 us
  between operations: 14.8 us -> 2.82 us
  local copies, waits for them, and re-layouts: 0.91 us -> 3.63 us
  other arithmetic: 2.36 us -> 3.49 us
    reduce_scatter x1 -> x0, waiting for transfers between devices: 25.1 us -> none  [per_device(): lax.psum_scatter(own_delta.astype(jnp.float32).astype(jnp.bfloat16), 'blk...]
    psum x1 -> x0, waiting for transfers between devices: 16.1 us -> none  [per_device(): summed = lax.psum(share_sum, ('rep', 'sub')).astype(jnp.float32)]
    ppermute x0 -> x10, waiting for transfers between devices: none -> 15.7 us  [swap(): return lax.ppermute(value, axis, [(i, i ^ bit) for i in range(size)])]
    all_gather x1 -> x0, blocking collectives: 14.1 us -> none  [per_device(): lax.all_gather(prev_master.astype(jnp.bfloat16), 'blk', axis=0, tiled=True)]
    ppermute x0 -> x10, starting transfers between devices: none -> 13.6 us  [swap(): return lax.ppermute(value, axis, [(i, i ^ bit) for i in range(size)])]
    psum x1 -> x0, blocking collectives: 12.7 us -> none  [per_device(): squares = lax.psum(jnp.sum(summed * summed), 'blk')]
    slice x0 -> x2, local copies, waits for them, and re-layouts: none -> 1.02 us  [per_device(): squares = squares + got[0, width]]
    convert_element_type x0 -> x2, local copies, waits for them, and re-layouts: none -> 0.99 us  [the longest x1 0.9 us: per_device(): prev = prev_master.astype(BF16)]
  transfers between devices with their start and end apart: 2 -> 10, of which waited for: 2 -> 7; matrix products, arithmetic and copies ran while one was open for 0% -> 6% of each run, Pallas kernels for 0% -> 0%
where the time goes in v1:
time: 39.5 us; the launch traced here: 39.2 us
  waiting for transfers between devices  15.7 us (40%)
  starting transfers between devices  13.6 us (34%)
  local copies, waits for them, and re-layouts  3.63 us (9%)
  other arithmetic  3.49 us (9%)
  between operations  2.82 us (7%)
    ppermute x10, waiting for transfers between devices, swap(): return lax.ppermute(value, axis, [(i, i ^ bit) for i in range(size)])  15.7 us
    ppermute x10, starting transfers between devices, swap(): return lax.ppermute(value, axis, [(i, i ^ bit) for i in range(size)])  13.6 us
    slice x2, local copies, waits for them, and re-layouts, per_device(): squares = squares + got[0, width]  1.02 us
    select_n x6, other arithmetic, joined(): jnp.where(upper, other, own)  0.98 us
    unnamed x6, local copies, waits for them, and re-layouts  0.95 us
    convert_element_type x1, local copies, waits for them, and re-layouts, per_device(): prev = prev_master.astype(BF16)  0.9 us
  transfers between devices with their start and end apart: 10, of which 7 were waited for; matrix products, arithmetic and copies ran while one was open for 6% of the time, Pallas kernels for 0%

profile of v1, /device:TPU:0, one launch (start us, length us, event | category | flops | bytes accessed | tf_op | source)
XLA Modules:
  0.0 39.2 jit_solution(9640844544530453084)
XLA Ops:
  0.6 0.0 copy-start
  0.7 0.9 %dynamic-slice_convert_fusion.1 = bf16[8,1152]{1,0:T(8,128)(2,1)S(1)} fusion(f32[8,4608]{1,0:T(8,128)} %param.7, s32[]{:T(128)S(6)} %dynamic_slice.21), kind=kLoop, calls=%fused_computation.22 | loop fusion | bytes 36868 | tf_op jit(solution)/shard_map/convert_element_type | solution.py:75
  1.6 3.1 %collective-permute-start.6 = (bf16[8,1152]{1,0:T(8,128)(2,1)S(1)}, bf16[8,1152]{1,0:T(8,128)(2,1)S(1)}, u32[]{:S(2)}, u32[]{:S(2)}) collective-permute-start(bf16[8,1152]{1,0:T(8,128)(2,1)S(1)} %dynamic-slice_convert_fusion.1), channel_id=1, source_target_pairs={{0,4},{4,0},{8,12},{12,8},{1,5},{5,1},{9,13},{13,9},{2,6},{6,2},{1... | collective-permute-start | bytes 55304 | tf_op jit(solution)/shard_map/ppermute | solution.py:14
  4.6 1.7 %collective-permute-done.6 = bf16[8,1152]{1,0:T(8,128)(2,1)S(1)} collective-permute-done((bf16[8,1152]{1,0:T(8,128)(2,1)S(1)}, bf16[8,1152]{1,0:T(8,128)(2,1)S(1)}, u32[]{:S(2)}, u32[]{:S(2)}) %collective-permute-start.6) | collective-permute-done | bytes 18464 | tf_op jit(solution)/shard_map/ppermute | solution.py:14
  6.4 0.9 %broadcast_select_fusion.7 = (bf16[8,1152]{1,0:T(8,128)(2,1)S(1)}, bf16[8,1152]{1,0:T(8,128)(2,1)S(1)}) fusion(bf16[8,1152]{1,0:T(8,128)(2,1)S(1)} %collective-permute-done.6, pred[]{:T(512)S(6)} %eq.28, f32[8,4608]{1,0:T(8,128)} %param.7, s32[]{:T(128)S(6)} %dynamic_slice.21), kind=kLoop, calls=%fused_computation.29 | loop fusion | flops 18432 | bytes 73733 | tf_op jit(solution)/shard_map/jit(_where)/select_n | solution.py:35
  7.2 3.1 %collective-permute-start.7 = (bf16[16,1152]{1,0:T(8,128)(2,1)S(1)}, bf16[16,1152]{1,0:T(8,128)(2,1)S(1)}, u32[]{:S(2)}, u32[]{:S(2)}) collective-permute-start(bf16[16,1152]{1,0:T(8,128)(2,1)S(1)} %pad_maximum_fusion.4), channel_id=1, source_target_pairs={{0,8},{4,12},{8,0},{12,4},{1,9},{5,13},{9,1},{13,5},{2,10},{6,14},... | collective-permute-start | bytes 110600 | tf_op jit(solution)/shard_map/ppermute | solution.py:14
  10.3 0.0 copy-done
  10.3 0.0 collective-permute-start
  10.3 1.9 %collective-permute-done.7 = bf16[16,1152]{1,0:T(8,128)(2,1)S(1)} collective-permute-done((bf16[16,1152]{1,0:T(8,128)(2,1)S(1)}, bf16[16,1152]{1,0:T(8,128)(2,1)S(1)}, u32[]{:S(2)}, u32[]{:S(2)}) %collective-permute-start.7) | collective-permute-done | bytes 36896 | tf_op jit(solution)/shard_map/ppermute | solution.py:14
  12.3 0.0 collective-permute-done
  12.3 0.1 convert_add_fusion
  12.4 0.1 dynamic-slice_convert_fusion
  12.5 1.9 %collective-permute-start.1 = (bf16[32,1152]{1,0:T(8,128)(2,1)S(1)}, bf16[32,1152]{1,0:T(8,128)(2,1)S(1)}, u32[]{:S(2)}, u32[]{:S(2)}) collective-permute-start(bf16[32,1152]{1,0:T(8,128)(2,1)S(1)} %dynamic-slice_convert_fusion), channel_id=1, source_target_pairs={{0,2},{2,0},{1,3},{3,1},{4,6},{6,4},{5,7},{7,5},{8,10},{10,8},{9,1... | collective-permute-start | bytes 221192 | tf_op jit(solution)/shard_map/ppermute | solution.py:14
  14.4 0.2 collective-permute-start.8
  14.6 3.1 %collective-permute-done.1 = bf16[32,1152]{1,0:T(8,128)(2,1)S(1)} collective-permute-done((bf16[32,1152]{1,0:T(8,128)(2,1)S(1)}, bf16[32,1152]{1,0:T(8,128)(2,1)S(1)}, u32[]{:S(2)}, u32[]{:S(2)}) %collective-permute-start.1) | collective-permute-done | bytes 73760 | tf_op jit(solution)/shard_map/ppermute | solution.py:14
  17.7 0.1 fusion.1
  17.8 1.6 %collective-permute-start.2 = (bf16[32,1152]{1,0:T(8,128)(2,1)S(1)}, bf16[32,1152]{1,0:T(8,128)(2,1)S(1)}, u32[]{:S(2)}, u32[]{:S(2)}) collective-permute-start(bf16[32,1152]{1,0:T(8,128)(2,1)S(1)} %fusion.1), channel_id=1, source_target_pairs={{0,4},{4,0},{8,12},{12,8},{1,5},{5,1},{9,13},{13,9},{2,6},{6,2},{1... | collective-permute-start | bytes 221192 | tf_op jit(solution)/shard_map/ppermute | solution.py:14
  19.4 0.0 collective-permute-done.8
  19.5 2.7 %collective-permute-done.2 = bf16[32,1152]{1,0:T(8,128)(2,1)S(1)} collective-permute-done((bf16[32,1152]{1,0:T(8,128)(2,1)S(1)}, bf16[32,1152]{1,0:T(8,128)(2,1)S(1)}, u32[]{:S(2)}, u32[]{:S(2)}) %collective-permute-start.2) | collective-permute-done | bytes 73760 | tf_op jit(solution)/shard_map/ppermute | solution.py:14
  22.2 0.1 fusion
  22.3 2.5 %collective-permute-start.3 = (bf16[32,1152]{1,0:T(8,128)(2,1)S(1)}, bf16[32,1152]{1,0:T(8,128)(2,1)S(1)}, u32[]{:S(2)}, u32[]{:S(2)}) collective-permute-start(bf16[32,1152]{1,0:T(8,128)(2,1)S(1)} %fusion), channel_id=1, source_target_pairs={{0,8},{4,12},{8,0},{12,4},{1,9},{5,13},{9,1},{13,5},{2,10},{6,14},... | collective-permute-start | bytes 221192 | tf_op jit(solution)/shard_map/ppermute | solution.py:14
  24.8 0.1 collective-permute-start.9
  24.9 2.8 %collective-permute-done.3 = bf16[32,1152]{1,0:T(8,128)(2,1)S(1)} collective-permute-done((bf16[32,1152]{1,0:T(8,128)(2,1)S(1)}, bf16[32,1152]{1,0:T(8,128)(2,1)S(1)}, u32[]{:S(2)}, u32[]{:S(2)}) %collective-permute-start.3) | collective-permute-done | bytes 73760 | tf_op jit(solution)/shard_map/ppermute | solution.py:14
  27.6 0.7 %multiply_reduce_fusion = (f32[]{:T(128)}, f32[32,1152]{1,0:T(8,128)S(1)}) fusion(bf16[32,1152]{1,0:T(8,128)(2,1)S(1)} %collective-permute-done.3, bf16[32,1152]{1,0:T(8,128)(2,1)S(1)} %collective-permute-done.2, bf16[32,1152]{1,0:T(8,128)(2,1)S(1)} %collective-permute-done.1, f32[32,4608]{1,0:T(8,128)S(1)} %convert_add_fusion, s32[]{:T(128)S(6)} %dynamic_slice.21), kind=kLoop, calls=%fused_computation.6 | loop fusion | flops 294911 | bytes 516104 | tf_op jit(solution)/shard_map/reduce_sum | solution.py:57
  28.4 0.6 %concatenate.25 = f32[8,1280]{1,0:T(8,128)S(1)} pad(f32[8,1152]{1,0:T(8,128)S(1)} %constant_dynamic-slice_fusion, f32[]{:T(128)} %get-tuple-element.5), padding=0_0x0_128 | pad | bytes 77828 | tf_op jit(solution)/shard_map/concatenate | solution.py:62
  29.0 1.1 %collective-permute-start.4 = (f32[8,1280]{1,0:T(8,128)S(1)}, f32[8,1280]{1,0:T(8,128)S(1)}, u32[]{:S(2)}, u32[]{:S(2)}) collective-permute-start(f32[8,1280]{1,0:T(8,128)S(1)} %concatenate.25), channel_id=1, source_target_pairs={{0,2},{2,0},{1,3},{3,1},{4,6},{6,4},{5,7},{7,5},{8,10},{10,8},{9,1... | collective-permute-start | bytes 122888 | tf_op jit(solution)/shard_map/ppermute | solution.py:14
  30.1 0.0 collective-permute-done.9
  30.2 0.1 broadcast_select_fusion.1
  30.2 2.9 %collective-permute-done.4 = f32[8,1280]{1,0:T(8,128)S(1)} collective-permute-done((f32[8,1280]{1,0:T(8,128)S(1)}, f32[8,1280]{1,0:T(8,128)S(1)}, u32[]{:S(2)}, u32[]{:S(2)}) %collective-permute-start.4) | collective-permute-done | bytes 40992 | tf_op jit(solution)/shard_map/ppermute | solution.py:14
  33.1 0.5 %slice.16 = f32[1,1]{1,0:T(1,128)} slice(f32[8,1280]{1,0:T(8,128)S(1)} %collective-permute-done.4), slice={[0:1], [1152:1153]} | slice | bytes 8 | tf_op jit(solution)/shard_map/slice | solution.py:66
  35.0 0.1 collective-permute-start.5
  35.0 0.7 %pad_maximum_fusion = bf16[32,4608]{1,0:T(8,128)(2,1)} fusion(bf16[32,2304]{1,0:T(8,128)(2,1)S(1)} %get-tuple-element.8, bf16[32,2304]{1,0:T(8,128)(2,1)S(1)} %get-tuple-element.7), kind=kLoop, calls=%fused_computation.1 | loop fusion | flops 589824 | bytes 589824 | tf_op jit(solution)/shard_map/concatenate | solution.py:34
  35.8 0.5 %collective-permute-done.5 = f32[8,2432]{1,0:T(8,128)S(1)} collective-permute-done((f32[8,2432]{1,0:T(8,128)S(1)}, f32[8,2432]{1,0:T(8,128)S(1)}, u32[]{:S(2)}, u32[]{:S(2)}) %collective-permute-start.5) | collective-permute-done | bytes 77856 | tf_op jit(solution)/shard_map/ppermute | solution.py:14
  36.3 0.5 %slice.18 = f32[1,1]{1,0:T(1,128)} slice(f32[8,2432]{1,0:T(8,128)S(1)} %collective-permute-done.5), slice={[0:1], [2304:2305]} | slice | bytes 8 | tf_op jit(solution)/shard_map/slice | solution.py:66
  37.5 0.0 copy-start.1
  37.5 0.0 copy-start.2
  37.6 0.9 %copy-done.1 = f32[8,4608]{1,0:T(8,128)S(1)} copy-done((f32[8,4608]{1,0:T(8,128)S(1)}, f32[8,4608]{1,0:T(8,128)}, u32[]{:S(2)}) %copy-start.1) | copy-done | bytes 147480
  38.4 0.1 copy-done.2
  38.5 0.7 %multiply_subtract_fusion = (f32[8,4608]{1,0:T(8,128)}, f32[8,4608]{1,0:T(8,128)}) fusion(f32[8,4608]{1,0:T(8,128)S(1)} %copy-done.1, f32[8,2304]{1,0:T(8,128)S(1)} %get-tuple-element.10, f32[8,2304]{1,0:T(8,128)S(1)} %get-tuple-element.9, f32[]{:T(128)S(6)} %min_shard_map.3, f32[8,4608]{1,0:T(8,128)S(1)} %copy-done.2), kind=kLoop, calls=%fused_computation.4 | loop fusion | flops 294912 | bytes 737284 | tf_op jit(solution)/shard_map/sub | solution.py:73
  (11 shorter events, 0.1 us)
Async XLA Ops:
  0.6 9.7 %copy-start = (bf16[1,32,4608]{2,1,0:T(8,128)(2,1)S(1)}, bf16[1,32,4608]{2,1,0:T(8,128)(2,1)}, u32[]{:S(2)}) copy-start(bf16[1,32,4608]{2,1,0:T(8,128)(2,1)} %param.4) | copy-start | bytes 884740
  1.6 4.8 %collective-permute-start.6 = (bf16[8,1152]{1,0:T(8,128)(2,1)S(1)}, bf16[8,1152]{1,0:T(8,128)(2,1)S(1)}, u32[]{:S(2)}, u32[]{:S(2)}) collective-permute-start(bf16[8,1152]{1,0:T(8,128)(2,1)S(1)} %dynamic-slice_convert_fusion.1), channel_id=1, source_target_pairs={{0,4},{4,0},{8,12},{12,8},{1,5},{5,1},{9,13},{13,9},{2,6},{6,2},{1... | collective-permute-start | bytes 55304 | tf_op jit(solution)/shard_map/ppermute | solution.py:14
  7.2 5.0 %collective-permute-start.7 = (bf16[16,1152]{1,0:T(8,128)(2,1)S(1)}, bf16[16,1152]{1,0:T(8,128)(2,1)S(1)}, u32[]{:S(2)}, u32[]{:S(2)}) collective-permute-start(bf16[16,1152]{1,0:T(8,128)(2,1)S(1)} %pad_maximum_fusion.4), channel_id=1, source_target_pairs={{0,8},{4,12},{8,0},{12,4},{1,9},{5,13},{9,1},{13,5},{2,10},{6,14},... | collective-permute-start | bytes 110600 | tf_op jit(solution)/shard_map/ppermute | solution.py:14
  10.3 2.0 %collective-permute-start = (bf16[32,4608]{1,0:T(8,128)(2,1)S(1)}, bf16[32,4608]{1,0:T(8,128)(2,1)S(1)}, u32[]{:S(2)}, u32[]{:S(2)}) collective-permute-start(bf16[32,4608]{1,0:T(8,128)(2,1)S(1)} %bitcast.4), channel_id=1, source_target_pairs={{0,1},{1,0},{2,3},{3,2},{4,5},{5,4},{6,7},{7,6},{8,9},{9,8},{10,11... | collective-permute-start | bytes 884744 | tf_op jit(solution)/shard_map/ppermute | solution.py:14
  12.5 5.2 %collective-permute-start.1 = (bf16[32,1152]{1,0:T(8,128)(2,1)S(1)}, bf16[32,1152]{1,0:T(8,128)(2,1)S(1)}, u32[]{:S(2)}, u32[]{:S(2)}) collective-permute-start(bf16[32,1152]{1,0:T(8,128)(2,1)S(1)} %dynamic-slice_convert_fusion), channel_id=1, source_target_pairs={{0,2},{2,0},{1,3},{3,1},{4,6},{6,4},{5,7},{7,5},{8,10},{10,8},{9,1... | collective-permute-start | bytes 221192 | tf_op jit(solution)/shard_map/ppermute | solution.py:14
  14.4 5.1 %collective-permute-start.8 = (bf16[32,1152]{1,0:T(8,128)(2,1)S(1)}, bf16[32,1152]{1,0:T(8,128)(2,1)S(1)}, u32[]{:S(2)}, u32[]{:S(2)}) collective-permute-start(bf16[32,1152]{1,0:T(8,128)(2,1)S(1)} %pad_maximum_fusion.3), channel_id=1, source_target_pairs={{0,2},{2,0},{1,3},{3,1},{4,6},{6,4},{5,7},{7,5},{8,10},{10,8},{9,1... | collective-permute-start | bytes 221192 | tf_op jit(solution)/shard_map/ppermute | solution.py:14
  17.8 4.4 %collective-permute-start.2 = (bf16[32,1152]{1,0:T(8,128)(2,1)S(1)}, bf16[32,1152]{1,0:T(8,128)(2,1)S(1)}, u32[]{:S(2)}, u32[]{:S(2)}) collective-permute-start(bf16[32,1152]{1,0:T(8,128)(2,1)S(1)} %fusion.1), channel_id=1, source_target_pairs={{0,4},{4,0},{8,12},{12,8},{1,5},{5,1},{9,13},{13,9},{2,6},{6,2},{1... | collective-permute-start | bytes 221192 | tf_op jit(solution)/shard_map/ppermute | solution.py:14
  22.3 5.3 %collective-permute-start.3 = (bf16[32,1152]{1,0:T(8,128)(2,1)S(1)}, bf16[32,1152]{1,0:T(8,128)(2,1)S(1)}, u32[]{:S(2)}, u32[]{:S(2)}) collective-permute-start(bf16[32,1152]{1,0:T(8,128)(2,1)S(1)} %fusion), channel_id=1, source_target_pairs={{0,8},{4,12},{8,0},{12,4},{1,9},{5,13},{9,1},{13,5},{2,10},{6,14},... | collective-permute-start | bytes 221192 | tf_op jit(solution)/shard_map/ppermute | solution.py:14
  24.8 5.3 %collective-permute-start.9 = (bf16[32,2304]{1,0:T(8,128)(2,1)S(1)}, bf16[32,2304]{1,0:T(8,128)(2,1)S(1)}, u32[]{:S(2)}, u32[]{:S(2)}) collective-permute-start(bf16[32,2304]{1,0:T(8,128)(2,1)S(1)} %pad_maximum_fusion.1), channel_id=1, source_target_pairs={{0,1},{1,0},{2,3},{3,2},{4,5},{5,4},{6,7},{7,6},{8,9},{9,8},{10,11... | collective-permute-start | bytes 442376 | tf_op jit(solution)/shard_map/ppermute | solution.py:14
  29.0 4.1 %collective-permute-start.4 = (f32[8,1280]{1,0:T(8,128)S(1)}, f32[8,1280]{1,0:T(8,128)S(1)}, u32[]{:S(2)}, u32[]{:S(2)}) collective-permute-start(f32[8,1280]{1,0:T(8,128)S(1)} %concatenate.25), channel_id=1, source_target_pairs={{0,2},{2,0},{1,3},{3,1},{4,6},{6,4},{5,7},{7,5},{8,10},{10,8},{9,1... | collective-permute-start | bytes 122888 | tf_op jit(solution)/shard_map/ppermute | solution.py:14
  35.0 1.3 %collective-permute-start.5 = (f32[8,2432]{1,0:T(8,128)S(1)}, f32[8,2432]{1,0:T(8,128)S(1)}, u32[]{:S(2)}, u32[]{:S(2)}) collective-permute-start(f32[8,2432]{1,0:T(8,128)S(1)} %maximum_maximum_fusion), channel_id=1, source_target_pairs={{0,1},{1,0},{2,3},{3,2},{4,5},{5,4},{6,7},{7,6},{8,9},{9,8},{10,11... | collective-permute-start | bytes 233480 | tf_op jit(solution)/shard_map/ppermute | solution.py:14
  37.5 0.9 %copy-start.1 = (f32[8,4608]{1,0:T(8,128)S(1)}, f32[8,4608]{1,0:T(8,128)}, u32[]{:S(2)}) copy-start(f32[8,4608]{1,0:T(8,128)} %param.6) | copy-start | bytes 442372
  37.5 1.0 %copy-start.2 = (f32[8,4608]{1,0:T(8,128)S(1)}, f32[8,4608]{1,0:T(8,128)}, u32[]{:S(2)}) copy-start(f32[8,4608]{1,0:T(8,128)} %param.5) | copy-start | bytes 442372

commit v2 on v0

v2 whole, which is shorter than its diff:
```python
import functools

import jax
import jax.numpy as jnp
from jax import lax
from jax.experimental import pallas as pl
from jax.experimental.pallas import tpu as pltpu
from jax.sharding import PartitionSpec as P

momentum_coef = 0.9
outer_rate = 0.7
F32 = jnp.float32
BF16 = jnp.bfloat16
LANES = 128
GROUP = ("blk", "rep", "sub")


def bits_of(size):
    return [1 << k for k in range(size.bit_length() - 1)]


def mine(axis, bit):
    return (lax.axis_index(axis) & bit) // bit


def halves(value, axis, bit):
    half = value.shape[1] // 2
    at = mine(axis, bit) * half
    keep = lax.dynamic_slice_in_dim(value, at, half, 1)
    away = lax.dynamic_slice_in_dim(value, half - at, half, 1)
    return keep, away


def joined(own, other, axis, bit, dim):
    upper = mine(axis, bit) == 1
    return jnp.concatenate(
        [jnp.where(upper, other, own), jnp.where(upper, own, other)], axis=dim
    )


def squares_of(total, rows):
    sq = total * total
    sq = jnp.pad(sq, ((0, 0), (0, -sq.shape[1] % LANES)))
    sq = sum(sq[:, k : k + LANES] for k in range(0, sq.shape[1], LANES))
    return jnp.sum(sq.reshape(-1, rows, LANES), axis=0)


def finish(entries, at_ref, own_ref, rep_ref, sub_ref, both_ref, m_ref, p_ref, np_ref, nm_ref, np_buf, nm_buf, sems):
    width = own_ref.shape[1] - 2 * LANES

    def squares(ref):
        return ref[:, width : width + LANES].astype(F32) + ref[:, width + LANES :].astype(F32)

    total = (squares(own_ref) + squares(rep_ref)) + (squares(sub_ref) + squares(both_ref))
    total = jnp.sum(jnp.sum(total, axis=0, keepdims=True), axis=1, keepdims=True)
    clip_factor = jnp.minimum(
        1.0, jnp.sqrt(jnp.full((1, 1), entries, F32)) / jnp.sqrt(total + 1e-06)
    )
    at = at_ref[0]
    for k, ref in enumerate((own_ref, rep_ref, sub_ref, both_ref)):
        cols = pl.ds(pl.multiple_of((at ^ k) * width, LANES), width)
        scaled = clip_factor * ref[:, :width].astype(F32)
        new_momentum = momentum_coef * m_ref[:, cols] + scaled
        nm_buf[:, cols] = new_momentum
        np_buf[:, cols] = p_ref[:, cols] - outer_rate * (scaled + momentum_coef * new_momentum)
    copies = [
        pltpu.make_async_copy(nm_buf, nm_ref, sems.at[0]),
        pltpu.make_async_copy(np_buf, np_ref, sems.at[1]),
    ]
    for copy in copies:
        copy.start()
    for copy in copies:
        copy.wait()


def make(mesh):
    n_blk, n_rep, n_sub = (mesh.shape[a] for a in GROUP)

    def swap(value, blk=0, rep=0, sub=0):
        pairs = []
        for i in range(n_blk * n_rep * n_sub):
            b, r, s = i // (n_rep * n_sub), i // n_sub % n_rep, i % n_sub
            pairs.append((i, ((b ^ blk) * n_rep + (r ^ rep)) * n_sub + (s ^ sub)))
        return lax.ppermute(value, GROUP, pairs)

    def per_device(replica_delta, momentum, params, prev_master):
        return step(replica_delta, momentum, params, prev_master)

    def step(replica_delta, momentum, params, prev_master):
        delta = replica_delta[0]
        rows, width = momentum.shape
        entries = delta.shape[0] * width

        other = swap(delta, sub=1)
        half, _ = halves(delta, "sub", 1)
        half = lax.optimization_barrier(half)
        prev = prev_master.astype(BF16)
        prev, _ = halves(prev, "sub", 1)
        other, prev = lax.optimization_barrier((other, prev))
        total = half.astype(F32) + halves(other, "sub", 1)[0].astype(F32)

        total, away = halves(total, "rep", 1)
        sent, away = total.astype(BF16), away.astype(BF16)
        got = (swap(away, rep=1), swap(sent, blk=1), swap(away, rep=1, blk=1))
        total = total + got[0].astype(F32) + got[1].astype(F32) + got[2].astype(F32)
        for bit in bits_of(n_rep)[1:]:
            total, away = halves(total, "rep", bit)
            total = total + swap(away.astype(BF16), rep=bit).astype(F32)
        for bit in bits_of(n_blk)[1:]:
            total = total + swap(total.astype(BF16), blk=bit).astype(F32)

        squares = squares_of(total, rows)
        own = lax.dynamic_slice_in_dim(total, lax.axis_index("blk") * rows, rows, 0).astype(BF16)

        def pack(own, squares):
            high = lax.reduce_precision(squares, 8, 7)
            return jnp.concatenate([own, high.astype(BF16), (squares - high).astype(BF16)], axis=1)

        for bit in reversed(bits_of(n_rep)[1:]):
            packed = swap(pack(own, squares), rep=bit)
            n = own.shape[1]
            own = joined(own, packed[:, :n], "rep", bit, 1)
            squares = squares + packed[:, n : n + LANES].astype(F32) + packed[:, n + LANES :].astype(F32)
        packed = pack(own, squares)
        from_rep = swap(packed, rep=1)
        from_sub = swap(packed, sub=1)
        from_both = swap(packed, rep=1, sub=1)

        for bit in reversed(bits_of(n_blk)):
            prev = joined(prev, swap(prev, blk=bit), "blk", bit, 0)
        order = [sum(((b >> k) & 1) * (n_blk >> (k + 1)) for k in range(n_blk.bit_length() - 1)) for b in range(n_blk)]
        prev = jnp.concatenate([prev[o * rows : (o + 1) * rows] for o in order], axis=0)
        prev_other = swap(prev, sub=1)
        prev = joined(prev, prev_other, "sub", 1, 1)

        at = (2 * lax.axis_index("sub") + mine("rep", 1)).reshape(1)
        vmem, hbm = pl.BlockSpec(memory_space=pltpu.VMEM), pl.BlockSpec(memory_space=pl.ANY)
        out = jax.ShapeDtypeStruct(params.shape, F32)
        new_params, new_momentum = pl.pallas_call(
            functools.partial(finish, float(entries)),
            out_shape=(out, out),
            in_specs=[pl.BlockSpec(memory_space=pltpu.SMEM)] + [vmem] * 6,
            out_specs=(hbm, hbm),
            scratch_shapes=[
                pltpu.VMEM(params.shape, F32),
                pltpu.VMEM(params.shape, F32),
                pltpu.SemaphoreType.DMA((2,)),
            ],
            compiler_params=pltpu.CompilerParams(vmem_limit_bytes=4 << 20),
        )(at, packed, from_rep, from_sub, from_both, momentum, params)
        return (new_params, new_momentum, prev)

    return per_device


def solution(mesh):
    in_specs = (
        P(("groups", "blk", "rep", "sub"), None, None),
        P(("groups", "blk"), None),
        P(("groups", "blk"), None),
        P(("groups", "blk"), None),
    )
    out_specs = (P(("groups", "blk"), None), P(("groups", "blk"), None), P("groups", None))
    return jax.shard_map(
        make(mesh), mesh=mesh, in_specs=in_specs, out_specs=out_specs, check_vma=False
    )
```

time: 87 us -> 27 us (0.31)
  waiting for transfers between devices: 41.9 us -> 10.6 us
  blocking collectives: 26.8 us -> 0 us
  between operations: 14.8 us -> 0.79 us
  starting transfers between devices: 0.08 us -> 12.6 us
  other arithmetic: 2.36 us -> 1.01 us
  Pallas kernels: 0 us -> 0.87 us
    reduce_scatter x1 -> x0, waiting for transfers between devices: 25.1 us -> none  [per_device(): lax.psum_scatter(own_delta.astype(jnp.float32).astype(jnp.bfloat16), 'blk...]
    psum x1 -> x0, waiting for transfers between devices: 16.1 us -> none  [per_device(): summed = lax.psum(share_sum, ('rep', 'sub')).astype(jnp.float32)]
    all_gather x1 -> x0, blocking collectives: 14.1 us -> none  [per_device(): lax.all_gather(prev_master.astype(jnp.bfloat16), 'blk', axis=0, tiled=True)]
    psum x1 -> x0, blocking collectives: 12.7 us -> none  [per_device(): squares = lax.psum(jnp.sum(summed * summed), 'blk')]
    ppermute x0 -> x11, starting transfers between devices: none -> 12.6 us  [swap(): return lax.ppermute(value, GROUP, pairs)]
    ppermute x0 -> x11, waiting for transfers between devices: none -> 10.6 us  [swap(): return lax.ppermute(value, GROUP, pairs)]
    reduce_sum x1, other arithmetic: 1.6 us -> 0.02 us  [squares_of(): return jnp.sum(sq.reshape(-1, rows, LANES), axis=0)]
    dynamic_slice x0 -> x1, local copies, waits for them, and re-layouts: none -> 0.92 us  [halves(): keep = lax.dynamic_slice_in_dim(value, at, half, 1)]
  transfers between devices with their start and end apart: 2 -> 11, of which waited for: 2 -> 7; matrix products, arithmetic and copies ran while one was open for 0% -> 5% of each run, Pallas kernels for 0% -> 3%
where the time goes in v2:
time: 27 us; the launch traced here: 26.9 us
  starting transfers between devices  12.6 us (47%)
  waiting for transfers between devices  10.6 us (39%)
  local copies, waits for them, and re-layouts  1.01 us (4%)
  other arithmetic  1.01 us (4%)
  Pallas kernels  0.87 us (3%)
  between operations  0.79 us (3%)
    ppermute x11, starting transfers between devices, swap(): return lax.ppermute(value, GROUP, pairs)  12.6 us
    ppermute x11, waiting for transfers between devices, swap(): return lax.ppermute(value, GROUP, pairs)  10.6 us
    dynamic_slice x1, local copies, waits for them, and re-layouts, halves(): keep = lax.dynamic_slice_in_dim(value, at, half, 1)  0.92 us
    pallas_call x1, Pallas kernels, step(): pl.pallas_call(functools.partial(finish, float(entries)), out_shape=(out,...  0.87 us
    concatenate x2, other arithmetic, joined(): jnp.concatenate([jnp.where(upper, other, own), jnp.where(upper, own, othe...  0.74 us
  transfers between devices with their start and end apart: 11, of which 7 were waited for; matrix products, arithmetic and copies ran while one was open for 5% of the time, Pallas kernels for 3%

profile of v2, /device:TPU:0, one launch (start us, length us, event | category | flops | bytes accessed | tf_op | source)
XLA Modules:
  0.0 26.9 jit_solution(11193498411128705330)
XLA Ops:
  0.6 0.0 copy-start
  0.6 0.6 %collective-permute-start = (bf16[32,4608]{1,0:T(8,128)(2,1)}, bf16[32,4608]{1,0:T(8,128)(2,1)S(1)}, u32[]{:S(2)}, u32[]{:S(2)}) collective-permute-start(bf16[32,4608]{1,0:T(8,128)(2,1)} %bitcast.8), channel_id=1, source_target_pairs={{0,1},{1,0},{2,3},{3,2},{4,5},{5,4},{6,7},{7,6},{8,9},{9,8},{10,11... | collective-permute-start | bytes 884744 | tf_op jit(solution)/shard_map/ppermute | solution.py:84
  1.2 0.9 %dynamic-slice_bitcast_fusion = bf16[32,2304]{1,0:T(8,128)(2,1)S(1)} fusion(bf16[1,32,4608]{2,1,0:T(8,128)(2,1)} %param.4, s32[]{:T(128)S(6)} %select_n.62), kind=kLoop, calls=%fused_computation.6 | loop fusion | bytes 294916 | tf_op jit(solution)/shard_map/dynamic_slice | solution.py:29
  2.1 0.0 copy-done
  2.2 0.4 %collective-permute-done = bf16[32,4608]{1,0:T(8,128)(2,1)S(1)} collective-permute-done((bf16[32,4608]{1,0:T(8,128)(2,1)}, bf16[32,4608]{1,0:T(8,128)(2,1)S(1)}, u32[]{:S(2)}, u32[]{:S(2)}) %collective-permute-start) | collective-permute-done | bytes 294944 | tf_op jit(solution)/shard_map/ppermute | solution.py:84
  2.6 3.9 %collective-permute-start.8 = (bf16[8,2304]{1,0:T(8,128)(2,1)S(1)}, bf16[8,2304]{1,0:T(8,128)(2,1)S(1)}, u32[]{:S(2)}, u32[]{:S(2)}) collective-permute-start(bf16[8,2304]{1,0:T(8,128)(2,1)S(1)} %dynamic-slice_convert_fusion.2), channel_id=1, source_target_pairs={{0,8},{1,9},{2,10},{3,11},{4,12},{5,13},{6,14},{7,15},{8,0},{9,1},... | collective-permute-start | bytes 110600 | tf_op jit(solution)/shard_map/ppermute | solution.py:84
  6.6 2.6 %collective-permute-start.3 = (bf16[32,1152]{1,0:T(8,128)(2,1)S(1)}, bf16[32,1152]{1,0:T(8,128)(2,1)S(1)}, u32[]{:S(2)}, u32[]{:S(2)}) collective-permute-start(bf16[32,1152]{1,0:T(8,128)(2,1)S(1)} %get-tuple-element.16), channel_id=1, source_target_pairs={{0,6},{1,7},{2,4},{3,5},{4,2},{5,3},{6,0},{7,1},{8,14},{9,15},{10,... | collective-permute-start | bytes 221192 | tf_op jit(solution)/shard_map/ppermute | solution.py:84
  9.2 0.5 %collective-permute-start.1 = (bf16[32,1152]{1,0:T(8,128)(2,1)S(1)}, bf16[32,1152]{1,0:T(8,128)(2,1)S(1)}, u32[]{:S(2)}, u32[]{:S(2)}) collective-permute-start(bf16[32,1152]{1,0:T(8,128)(2,1)S(1)} %get-tuple-element.16), channel_id=1, source_target_pairs={{0,2},{1,3},{2,0},{3,1},{4,6},{5,7},{6,4},{7,5},{8,10},{9,11},{10,... | collective-permute-start | bytes 221192 | tf_op jit(solution)/shard_map/ppermute | solution.py:84
  9.7 0.4 %collective-permute-start.2 = (bf16[32,1152]{1,0:T(8,128)(2,1)S(1)}, bf16[32,1152]{1,0:T(8,128)(2,1)S(1)}, u32[]{:S(2)}, u32[]{:S(2)}) collective-permute-start(bf16[32,1152]{1,0:T(8,128)(2,1)S(1)} %get-tuple-element.15), channel_id=1, source_target_pairs={{0,4},{1,5},{2,6},{3,7},{4,0},{5,1},{6,2},{7,3},{8,12},{9,13},{10,... | collective-permute-start | bytes 221192 | tf_op jit(solution)/shard_map/ppermute | solution.py:84
  10.2 0.0 collective-permute-done.8
  10.2 1.6 %collective-permute-start.9 = (bf16[16,2304]{1,0:T(8,128)(2,1)S(1)}, bf16[16,2304]{1,0:T(8,128)(2,1)S(1)}, u32[]{:S(2)}, u32[]{:S(2)}) collective-permute-start(bf16[16,2304]{1,0:T(8,128)(2,1)S(1)} %pad_maximum_fusion.2), channel_id=1, source_target_pairs={{0,4},{1,5},{2,6},{3,7},{4,0},{5,1},{6,2},{7,3},{8,12},{9,13},{10,... | collective-permute-start | bytes 221192 | tf_op jit(solution)/shard_map/ppermute | solution.py:84
  11.9 0.1 collective-permute-done.3
  12.0 2.3 %collective-permute-done.2 = bf16[32,1152]{1,0:T(8,128)(2,1)S(1)} collective-permute-done((bf16[32,1152]{1,0:T(8,128)(2,1)S(1)}, bf16[32,1152]{1,0:T(8,128)(2,1)S(1)}, u32[]{:S(2)}, u32[]{:S(2)}) %collective-permute-start.2) | collective-permute-done | bytes 73760 | tf_op jit(solution)/shard_map/ppermute | solution.py:84
  14.4 0.0 collective-permute-done.1
  14.4 0.6 %collective-permute-start.4 = (bf16[32,1152]{1,0:T(8,128)(2,1)S(1)}, bf16[32,1152]{1,0:T(8,128)(2,1)S(1)}, u32[]{:S(2)}, u32[]{:S(2)}) collective-permute-start(bf16[32,1152]{1,0:T(8,128)(2,1)S(1)} %fusion.3), channel_id=1, source_target_pairs={{0,8},{1,9},{2,10},{3,11},{4,12},{5,13},{6,14},{7,15},{8,0},{9,1},... | collective-permute-start | bytes 221192 | tf_op jit(solution)/shard_map/ppermute | solution.py:84
  15.0 0.1 collective-permute-done.9
  15.2 0.1 collective-permute-start.10
  15.3 4.4 %collective-permute-done.4 = bf16[32,1152]{1,0:T(8,128)(2,1)S(1)} collective-permute-done((bf16[32,1152]{1,0:T(8,128)(2,1)S(1)}, bf16[32,1152]{1,0:T(8,128)(2,1)S(1)}, u32[]{:S(2)}, u32[]{:S(2)}) %collective-permute-start.4) | collective-permute-done | bytes 73760 | tf_op jit(solution)/shard_map/ppermute | solution.py:84
  19.7 0.0 copy-start.2
  19.7 0.1 fusion.4
  19.8 0.0 copy-start.1
  19.9 2.1 %collective-permute-start.5 = (bf16[8,1408]{1,0:T(8,128)(2,1)S(1)}, bf16[8,1408]{1,0:T(8,128)(2,1)S(1)}, u32[]{:S(2)}, u32[]{:S(2)}) collective-permute-start(bf16[8,1408]{1,0:T(8,128)(2,1)S(1)} %pad_maximum_fusion.3.own_ref), channel_id=1, source_target_pairs={{0,2},{1,3},{2,0},{3,1},{4,6},{5,7},{6,4},{7,5},{8,10},{9,11},{10,... | collective-permute-start | bytes 67592 | tf_op jit(solution)/shard_map/ppermute | solution.py:84
  22.0 0.0 collective-permute-start.6
  22.0 0.2 collective-permute-start.7
  22.1 1.6 %collective-permute-done.5.rep_ref = bf16[8,1408]{1,0:T(8,128)(2,1)S(1)} collective-permute-done((bf16[8,1408]{1,0:T(8,128)(2,1)S(1)}, bf16[8,1408]{1,0:T(8,128)(2,1)S(1)}, u32[]{:S(2)}, u32[]{:S(2)}) %collective-permute-start.5) | collective-permute-done | bytes 22560 | tf_op jit(solution)/shard_map/ppermute | solution.py:84
  23.7 0.0 collective-permute-done.6.sub_ref
  23.7 1.4 %collective-permute-done.7.both_ref = bf16[8,1408]{1,0:T(8,128)(2,1)S(1)} collective-permute-done((bf16[8,1408]{1,0:T(8,128)(2,1)S(1)}, bf16[8,1408]{1,0:T(8,128)(2,1)S(1)}, u32[]{:S(2)}, u32[]{:S(2)}) %collective-permute-start.7) | collective-permute-done | bytes 22560 | tf_op jit(solution)/shard_map/ppermute | solution.py:84
  25.2 0.0 copy-done.2
  25.2 0.0 copy-done.1
  25.2 0.9 %shard_map.67 = (f32[8,4608]{1,0:T(8,128)}, f32[8,4608]{1,0:T(8,128)}) custom-call(s32[1]{0:T(128)} %bitcast.at_ref, bf16[8,1408]{1,0:T(8,128)(2,1)S(1)} %pad_maximum_fusion.3.own_ref, bf16[8,1408]{1,0:T(8,128)(2,1)S(1)} %collective-permute-done.5.rep_ref, bf16[8,1408]{1,0:T(8,128)(2,1)S(1)} %collective-permute-done.6.sub_ref, ...), custom_call_target="tpu_custom_call" | custom-call | tf_op jit(solution)/shard_map/pallas_call | solution.py:139
  26.1 0.0 collective-permute-done.10
  26.1 0.1 broadcast_select_fusion.1
  26.1 0.7 %pad_maximum_fusion = bf16[32,4608]{1,0:T(8,128)(2,1)} fusion(bf16[32,2304]{1,0:T(8,128)(2,1)S(1)} %get-tuple-element.14, bf16[32,2304]{1,0:T(8,128)(2,1)S(1)} %get-tuple-element.13), kind=kLoop, calls=%fused_computation | loop fusion | flops 589824 | bytes 589824 | tf_op jit(solution)/shard_map/concatenate | solution.py:36
  (13 shorter events, 0.2 us)
Async XLA Ops:
  0.6 1.5 %copy-start = (f32[8,4608]{1,0:T(8,128)S(1)}, f32[8,4608]{1,0:T(8,128)}, u32[]{:S(2)}) copy-start(f32[8,4608]{1,0:T(8,128)} %param.7) | copy-start | bytes 442372
  0.6 2.0 %collective-permute-start = (bf16[32,4608]{1,0:T(8,128)(2,1)}, bf16[32,4608]{1,0:T(8,128)(2,1)S(1)}, u32[]{:S(2)}, u32[]{:S(2)}) collective-permute-start(bf16[32,4608]{1,0:T(8,128)(2,1)} %bitcast.8), channel_id=1, source_target_pairs={{0,1},{1,0},{2,3},{3,2},{4,5},{5,4},{6,7},{7,6},{8,9},{9,8},{10,11... | collective-permute-start | bytes 884744 | tf_op jit(solution)/shard_map/ppermute | solution.py:84
  2.6 7.6 %collective-permute-start.8 = (bf16[8,2304]{1,0:T(8,128)(2,1)S(1)}, bf16[8,2304]{1,0:T(8,128)(2,1)S(1)}, u32[]{:S(2)}, u32[]{:S(2)}) collective-permute-start(bf16[8,2304]{1,0:T(8,128)(2,1)S(1)} %dynamic-slice_convert_fusion.2), channel_id=1, source_target_pairs={{0,8},{1,9},{2,10},{3,11},{4,12},{5,13},{6,14},{7,15},{8,0},{9,1},... | collective-permute-start | bytes 110600 | tf_op jit(solution)/shard_map/ppermute | solution.py:84
  6.6 5.4 %collective-permute-start.3 = (bf16[32,1152]{1,0:T(8,128)(2,1)S(1)}, bf16[32,1152]{1,0:T(8,128)(2,1)S(1)}, u32[]{:S(2)}, u32[]{:S(2)}) collective-permute-start(bf16[32,1152]{1,0:T(8,128)(2,1)S(1)} %get-tuple-element.16), channel_id=1, source_target_pairs={{0,6},{1,7},{2,4},{3,5},{4,2},{5,3},{6,0},{7,1},{8,14},{9,15},{10,... | collective-permute-start | bytes 221192 | tf_op jit(solution)/shard_map/ppermute | solution.py:84
  9.2 5.1 %collective-permute-start.1 = (bf16[32,1152]{1,0:T(8,128)(2,1)S(1)}, bf16[32,1152]{1,0:T(8,128)(2,1)S(1)}, u32[]{:S(2)}, u32[]{:S(2)}) collective-permute-start(bf16[32,1152]{1,0:T(8,128)(2,1)S(1)} %get-tuple-element.16), channel_id=1, source_target_pairs={{0,2},{1,3},{2,0},{3,1},{4,6},{5,7},{6,4},{7,5},{8,10},{9,11},{10,... | collective-permute-start | bytes 221192 | tf_op jit(solution)/shard_map/ppermute | solution.py:84
  9.7 4.6 %collective-permute-start.2 = (bf16[32,1152]{1,0:T(8,128)(2,1)S(1)}, bf16[32,1152]{1,0:T(8,128)(2,1)S(1)}, u32[]{:S(2)}, u32[]{:S(2)}) collective-permute-start(bf16[32,1152]{1,0:T(8,128)(2,1)S(1)} %get-tuple-element.15), channel_id=1, source_target_pairs={{0,4},{1,5},{2,6},{3,7},{4,0},{5,1},{6,2},{7,3},{8,12},{9,13},{10,... | collective-permute-start | bytes 221192 | tf_op jit(solution)/shard_map/ppermute | solution.py:84
  10.2 4.9 %collective-permute-start.9 = (bf16[16,2304]{1,0:T(8,128)(2,1)S(1)}, bf16[16,2304]{1,0:T(8,128)(2,1)S(1)}, u32[]{:S(2)}, u32[]{:S(2)}) collective-permute-start(bf16[16,2304]{1,0:T(8,128)(2,1)S(1)} %pad_maximum_fusion.2), channel_id=1, source_target_pairs={{0,4},{1,5},{2,6},{3,7},{4,0},{5,1},{6,2},{7,3},{8,12},{9,13},{10,... | collective-permute-start | bytes 221192 | tf_op jit(solution)/shard_map/ppermute | solution.py:84
  14.4 5.3 %collective-permute-start.4 = (bf16[32,1152]{1,0:T(8,128)(2,1)S(1)}, bf16[32,1152]{1,0:T(8,128)(2,1)S(1)}, u32[]{:S(2)}, u32[]{:S(2)}) collective-permute-start(bf16[32,1152]{1,0:T(8,128)(2,1)S(1)} %fusion.3), channel_id=1, source_target_pairs={{0,8},{1,9},{2,10},{3,11},{4,12},{5,13},{6,14},{7,15},{8,0},{9,1},... | collective-permute-start | bytes 221192 | tf_op jit(solution)/shard_map/ppermute | solution.py:84
  15.2 10.8 %collective-permute-start.10 = (bf16[32,2304]{1,0:T(8,128)(2,1)S(1)}, bf16[32,2304]{1,0:T(8,128)(2,1)S(1)}, u32[]{:S(2)}, u32[]{:S(2)}) collective-permute-start(bf16[32,2304]{1,0:T(8,128)(2,1)S(1)} %pad_maximum_fusion.1), channel_id=1, source_target_pairs={{0,1},{1,0},{2,3},{3,2},{4,5},{5,4},{6,7},{7,6},{8,9},{9,8},{10,11... | collective-permute-start | bytes 442376 | tf_op jit(solution)/shard_map/ppermute | solution.py:84
  19.7 5.5 %copy-start.2 = (f32[8,4608]{1,0:T(8,128)S(1)}, f32[8,4608]{1,0:T(8,128)}, u32[]{:S(2)}) copy-start(f32[8,4608]{1,0:T(8,128)} %p_ref.1) | copy-start | bytes 442372
  19.8 5.4 %copy-start.1 = (f32[8,4608]{1,0:T(8,128)S(1)}, f32[8,4608]{1,0:T(8,128)}, u32[]{:S(2)}) copy-start(f32[8,4608]{1,0:T(8,128)} %m_ref.1) | copy-start | bytes 442372
  19.9 3.9 %collective-permute-start.5 = (bf16[8,1408]{1,0:T(8,128)(2,1)S(1)}, bf16[8,1408]{1,0:T(8,128)(2,1)S(1)}, u32[]{:S(2)}, u32[]{:S(2)}) collective-permute-start(bf16[8,1408]{1,0:T(8,128)(2,1)S(1)} %pad_maximum_fusion.3.own_ref), channel_id=1, source_target_pairs={{0,2},{1,3},{2,0},{3,1},{4,6},{5,7},{6,4},{7,5},{8,10},{9,11},{10,... | collective-permute-start | bytes 67592 | tf_op jit(solution)/shard_map/ppermute | solution.py:84
  22.0 1.8 %collective-permute-start.6 = (bf16[8,1408]{1,0:T(8,128)(2,1)S(1)}, bf16[8,1408]{1,0:T(8,128)(2,1)S(1)}, u32[]{:S(2)}, u32[]{:S(2)}) collective-permute-start(bf16[8,1408]{1,0:T(8,128)(2,1)S(1)} %pad_maximum_fusion.3.own_ref), channel_id=1, source_target_pairs={{0,1},{1,0},{2,3},{3,2},{4,5},{5,4},{6,7},{7,6},{8,9},{9,8},{10,11... | collective-permute-start | bytes 67592 | tf_op jit(solution)/shard_map/ppermute | solution.py:84
  22.0 3.2 %collective-permute-start.7 = (bf16[8,1408]{1,0:T(8,128)(2,1)S(1)}, bf16[8,1408]{1,0:T(8,128)(2,1)S(1)}, u32[]{:S(2)}, u32[]{:S(2)}) collective-permute-start(bf16[8,1408]{1,0:T(8,128)(2,1)S(1)} %pad_maximum_fusion.3.own_ref), channel_id=1, source_target_pairs={{0,3},{1,2},{2,1},{3,0},{4,7},{5,6},{6,5},{7,4},{8,11},{9,10},{10,... | collective-permute-start | bytes 67592 | tf_op jit(solution)/shard_map/ppermute | solution.py:84

commit v3 on v2

--- a/solution.py
+++ b/solution.py
@@ -45,7 +45,7 @@
     return jnp.sum(sq.reshape(-1, rows, LANES), axis=0)
 
 
-def finish(entries, at_ref, own_ref, rep_ref, sub_ref, both_ref, m_ref, p_ref, np_ref, nm_ref, np_buf, nm_buf, sems):
+def finish(entries, at_ref, own_ref, rep_ref, sub_ref, both_ref, base_m_ref, base_p_ref, np_ref, nm_ref, np_buf, nm_buf, sems):
     width = own_ref.shape[1] - 2 * LANES
 
     def squares(ref):
@@ -57,18 +57,15 @@
         1.0, jnp.sqrt(jnp.full((1, 1), entries, F32)) / jnp.sqrt(total + 1e-06)
     )
     at = at_ref[0]
+    copies = []
     for k, ref in enumerate((own_ref, rep_ref, sub_ref, both_ref)):
         cols = pl.ds(pl.multiple_of((at ^ k) * width, LANES), width)
         scaled = clip_factor * ref[:, :width].astype(F32)
-        new_momentum = momentum_coef * m_ref[:, cols] + scaled
-        nm_buf[:, cols] = new_momentum
-        np_buf[:, cols] = p_ref[:, cols] - outer_rate * (scaled + momentum_coef * new_momentum)
-    copies = [
-        pltpu.make_async_copy(nm_buf, nm_ref, sems.at[0]),
-        pltpu.make_async_copy(np_buf, np_ref, sems.at[1]),
-    ]
-    for copy in copies:
-        copy.start()
+        nm_buf[:, cols] = base_m_ref[:, cols] + scaled
+        np_buf[:, cols] = base_p_ref[:, cols] - outer_rate * (1.0 + momentum_coef) * scaled
+        for j, (buf, ref) in enumerate(((nm_buf, nm_ref), (np_buf, np_ref))):
+            copies.append(pltpu.make_async_copy(buf.at[:, cols], ref.at[:, cols], sems.at[2 * k + j]))
+            copies[-1].start()
     for copy in copies:
         copy.wait()
 
@@ -107,7 +104,9 @@
             total, away = halves(total, "rep", bit)
             total = total + swap(away.astype(BF16), rep=bit).astype(F32)
         for bit in bits_of(n_blk)[1:]:
-            total = total + swap(total.astype(BF16), blk=bit).astype(F32)
+            sent = total.astype(BF16)
+            got_far = swap(sent, blk=bit)
+            total = total + got_far.astype(F32)
 
         squares = squares_of(total, rows)
         own = lax.dynamic_slice_in_dim(total, lax.axis_index("blk") * rows, rows, 0).astype(BF16)
@@ -133,6 +132,8 @@
         prev_other = swap(prev, sub=1)
         prev = joined(prev, prev_other, "sub", 1, 1)
 
+        base_m = momentum_coef * momentum
+        base_p = params - outer_rate * momentum_coef * base_m
         at = (2 * lax.axis_index("sub") + mine("rep", 1)).reshape(1)
         vmem, hbm = pl.BlockSpec(memory_space=pltpu.VMEM), pl.BlockSpec(memory_space=pl.ANY)
         out = jax.ShapeDtypeStruct(params.shape, F32)
@@ -144,10 +145,10 @@
             scratch_shapes=[
                 pltpu.VMEM(params.shape, F32),
                 pltpu.VMEM(params.shape, F32),
-                pltpu.SemaphoreType.DMA((2,)),
+                pltpu.SemaphoreType.DMA((8,)),
             ],
             compiler_params=pltpu.CompilerParams(vmem_limit_bytes=4 << 20),
-        )(at, packed, from_rep, from_sub, from_both, momentum, params)
+        )(at, packed, from_rep, from_sub, from_both, base_m, base_p)
         return (new_params, new_momentum, prev)
 
     return per_device

time: 27 us -> 27 us (level)
  no operation moved by 1% of the time
where the time goes in v3:
time: 27 us; the launch traced here: 26.9 us
  starting transfers between devices  12.6 us (47%)
  waiting for transfers between devices  10.5 us (39%)
  other arithmetic  1.03 us (4%)
  local copies, waits for them, and re-layouts  1.01 us (4%)
  Pallas kernels  0.89 us (3%)
  between operations  0.8 us (3%)
    ppermute x11, starting transfers between devices, swap(): return lax.ppermute(value, GROUP, pairs)  12.6 us
    ppermute x11, waiting for transfers between devices, swap(): return lax.ppermute(value, GROUP, pairs)  10.5 us
    dynamic_slice x1, local copies, waits for them, and re-layouts, halves(): keep = lax.dynamic_slice_in_dim(value, at, half, 1)  0.92 us
    pallas_call x1, Pallas kernels, step(): pl.pallas_call(functools.partial(finish, float(entries)), out_shape=(out,...  0.89 us
    concatenate x2, other arithmetic, joined(): jnp.concatenate([jnp.where(upper, other, own), jnp.where(upper, own, othe...  0.74 us
  transfers between devices with their start and end apart: 11, of which 7 were waited for; matrix products, arithmetic and copies ran while one was open for 5% of the time, Pallas kernels for 3%

profile of v3, /device:TPU:0, one launch (start us, length us, event | category | flops | bytes accessed | tf_op | source)
XLA Modules:
  0.0 26.9 jit_solution(11633936048042195215)
XLA Ops:
  0.6 0.0 copy-start
  0.6 0.6 %collective-permute-start = (bf16[32,4608]{1,0:T(8,128)(2,1)}, bf16[32,4608]{1,0:T(8,128)(2,1)S(1)}, u32[]{:S(2)}, u32[]{:S(2)}) collective-permute-start(bf16[32,4608]{1,0:T(8,128)(2,1)} %bitcast.8), channel_id=1, source_target_pairs={{0,1},{1,0},{2,3},{3,2},{4,5},{5,4},{6,7},{7,6},{8,9},{9,8},{10,11... | collective-permute-start | bytes 884744 | tf_op jit(solution)/shard_map/ppermute | solution.py:81
  1.2 0.9 %dynamic-slice_bitcast_fusion = bf16[32,2304]{1,0:T(8,128)(2,1)S(1)} fusion(bf16[1,32,4608]{2,1,0:T(8,128)(2,1)} %param.4, s32[]{:T(128)S(6)} %select_n.62), kind=kLoop, calls=%fused_computation.7 | loop fusion | bytes 294916 | tf_op jit(solution)/shard_map/dynamic_slice | solution.py:29
  2.1 0.0 copy-done
  2.2 0.4 %collective-permute-done = bf16[32,4608]{1,0:T(8,128)(2,1)S(1)} collective-permute-done((bf16[32,4608]{1,0:T(8,128)(2,1)}, bf16[32,4608]{1,0:T(8,128)(2,1)S(1)}, u32[]{:S(2)}, u32[]{:S(2)}) %collective-permute-start) | collective-permute-done | bytes 294944 | tf_op jit(solution)/shard_map/ppermute | solution.py:81
  2.6 3.9 %collective-permute-start.8 = (bf16[8,2304]{1,0:T(8,128)(2,1)S(1)}, bf16[8,2304]{1,0:T(8,128)(2,1)S(1)}, u32[]{:S(2)}, u32[]{:S(2)}) collective-permute-start(bf16[8,2304]{1,0:T(8,128)(2,1)S(1)} %dynamic-slice_convert_fusion.2), channel_id=1, source_target_pairs={{0,8},{1,9},{2,10},{3,11},{4,12},{5,13},{6,14},{7,15},{8,0},{9,1},... | collective-permute-start | bytes 110600 | tf_op jit(solution)/shard_map/ppermute | solution.py:81
  6.6 2.6 %collective-permute-start.3 = (bf16[32,1152]{1,0:T(8,128)(2,1)S(1)}, bf16[32,1152]{1,0:T(8,128)(2,1)S(1)}, u32[]{:S(2)}, u32[]{:S(2)}) collective-permute-start(bf16[32,1152]{1,0:T(8,128)(2,1)S(1)} %get-tuple-element.16), channel_id=1, source_target_pairs={{0,6},{1,7},{2,4},{3,5},{4,2},{5,3},{6,0},{7,1},{8,14},{9,15},{10,... | collective-permute-start | bytes 221192 | tf_op jit(solution)/shard_map/ppermute | solution.py:81
  9.2 0.5 %collective-permute-start.1 = (bf16[32,1152]{1,0:T(8,128)(2,1)S(1)}, bf16[32,1152]{1,0:T(8,128)(2,1)S(1)}, u32[]{:S(2)}, u32[]{:S(2)}) collective-permute-start(bf16[32,1152]{1,0:T(8,128)(2,1)S(1)} %get-tuple-element.16), channel_id=1, source_target_pairs={{0,2},{1,3},{2,0},{3,1},{4,6},{5,7},{6,4},{7,5},{8,10},{9,11},{10,... | collective-permute-start | bytes 221192 | tf_op jit(solution)/shard_map/ppermute | solution.py:81
  9.7 0.4 %collective-permute-start.2 = (bf16[32,1152]{1,0:T(8,128)(2,1)S(1)}, bf16[32,1152]{1,0:T(8,128)(2,1)S(1)}, u32[]{:S(2)}, u32[]{:S(2)}) collective-permute-start(bf16[32,1152]{1,0:T(8,128)(2,1)S(1)} %get-tuple-element.15), channel_id=1, source_target_pairs={{0,4},{1,5},{2,6},{3,7},{4,0},{5,1},{6,2},{7,3},{8,12},{9,13},{10,... | collective-permute-start | bytes 221192 | tf_op jit(solution)/shard_map/ppermute | solution.py:81
  10.2 0.0 collective-permute-done.8
  10.2 1.6 %collective-permute-start.9 = (bf16[16,2304]{1,0:T(8,128)(2,1)S(1)}, bf16[16,2304]{1,0:T(8,128)(2,1)S(1)}, u32[]{:S(2)}, u32[]{:S(2)}) collective-permute-start(bf16[16,2304]{1,0:T(8,128)(2,1)S(1)} %pad_maximum_fusion.2), channel_id=1, source_target_pairs={{0,4},{1,5},{2,6},{3,7},{4,0},{5,1},{6,2},{7,3},{8,12},{9,13},{10,... | collective-permute-start | bytes 221192 | tf_op jit(solution)/shard_map/ppermute | solution.py:81
  11.9 0.1 collective-permute-done.3
  12.0 2.3 %collective-permute-done.2 = bf16[32,1152]{1,0:T(8,128)(2,1)S(1)} collective-permute-done((bf16[32,1152]{1,0:T(8,128)(2,1)S(1)}, bf16[32,1152]{1,0:T(8,128)(2,1)S(1)}, u32[]{:S(2)}, u32[]{:S(2)}) %collective-permute-start.2) | collective-permute-done | bytes 73760 | tf_op jit(solution)/shard_map/ppermute | solution.py:81
  14.4 0.0 collective-permute-done.1
  14.4 0.6 %collective-permute-start.4 = (bf16[32,1152]{1,0:T(8,128)(2,1)S(1)}, bf16[32,1152]{1,0:T(8,128)(2,1)S(1)}, u32[]{:S(2)}, u32[]{:S(2)}) collective-permute-start(bf16[32,1152]{1,0:T(8,128)(2,1)S(1)} %fusion.3), channel_id=1, source_target_pairs={{0,8},{1,9},{2,10},{3,11},{4,12},{5,13},{6,14},{7,15},{8,0},{9,1},... | collective-permute-start | bytes 221192 | tf_op jit(solution)/shard_map/ppermute | solution.py:81
  15.0 0.1 collective-permute-done.9
  15.2 0.1 collective-permute-start.10
  15.3 4.4 %collective-permute-done.4 = bf16[32,1152]{1,0:T(8,128)(2,1)S(1)} collective-permute-done((bf16[32,1152]{1,0:T(8,128)(2,1)S(1)}, bf16[32,1152]{1,0:T(8,128)(2,1)S(1)}, u32[]{:S(2)}, u32[]{:S(2)}) %collective-permute-start.4) | collective-permute-done | bytes 73760 | tf_op jit(solution)/shard_map/ppermute | solution.py:81
  19.7 0.0 copy-start.2
  19.7 0.1 fusion.4
  19.8 0.0 copy-start.1
  19.9 2.1 %collective-permute-start.5 = (bf16[8,1408]{1,0:T(8,128)(2,1)S(1)}, bf16[8,1408]{1,0:T(8,128)(2,1)S(1)}, u32[]{:S(2)}, u32[]{:S(2)}) collective-permute-start(bf16[8,1408]{1,0:T(8,128)(2,1)S(1)} %pad_maximum_fusion.3.own_ref), channel_id=1, source_target_pairs={{0,2},{1,3},{2,0},{3,1},{4,6},{5,7},{6,4},{7,5},{8,10},{9,11},{10,... | collective-permute-start | bytes 67592 | tf_op jit(solution)/shard_map/ppermute | solution.py:81
  22.0 0.0 collective-permute-start.6
  22.0 0.2 collective-permute-start.7
  22.1 0.0 copy-done.2
  22.1 0.0 copy-done.1
  22.2 1.6 %collective-permute-done.5.rep_ref = bf16[8,1408]{1,0:T(8,128)(2,1)S(1)} collective-permute-done((bf16[8,1408]{1,0:T(8,128)(2,1)S(1)}, bf16[8,1408]{1,0:T(8,128)(2,1)S(1)}, u32[]{:S(2)}, u32[]{:S(2)}) %collective-permute-start.5) | collective-permute-done | bytes 22560 | tf_op jit(solution)/shard_map/ppermute | solution.py:81
  23.7 0.0 collective-permute-done.6.sub_ref
  23.7 1.4 %collective-permute-done.7.both_ref = bf16[8,1408]{1,0:T(8,128)(2,1)S(1)} collective-permute-done((bf16[8,1408]{1,0:T(8,128)(2,1)S(1)}, bf16[8,1408]{1,0:T(8,128)(2,1)S(1)}, u32[]{:S(2)}, u32[]{:S(2)}) %collective-permute-start.7) | collective-permute-done | bytes 22560 | tf_op jit(solution)/shard_map/ppermute | solution.py:81
  25.2 0.9 %shard_map.67 = (f32[8,4608]{1,0:T(8,128)}, f32[8,4608]{1,0:T(8,128)}) custom-call(s32[1]{0:T(128)} %bitcast.at_ref, bf16[8,1408]{1,0:T(8,128)(2,1)S(1)} %pad_maximum_fusion.3.own_ref, bf16[8,1408]{1,0:T(8,128)(2,1)S(1)} %collective-permute-done.5.rep_ref, bf16[8,1408]{1,0:T(8,128)(2,1)S(1)} %collective-permute-done.6.sub_ref, ...), custom_call_target="tpu_custom_call" | custom-call | tf_op jit(solution)/shard_map/pallas_call | solution.py:140
  26.1 0.0 collective-permute-done.10
  26.1 0.1 broadcast_select_fusion.1
  26.2 0.7 %pad_maximum_fusion = bf16[32,4608]{1,0:T(8,128)(2,1)} fusion(bf16[32,2304]{1,0:T(8,128)(2,1)S(1)} %get-tuple-element.14, bf16[32,2304]{1,0:T(8,128)(2,1)S(1)} %get-tuple-element.13), kind=kLoop, calls=%fused_computation | loop fusion | flops 589824 | bytes 589824 | tf_op jit(solution)/shard_map/concatenate | solution.py:36
  (14 shorter events, 0.3 us)
Async XLA Ops:
  0.6 1.5 %copy-start = (f32[8,4608]{1,0:T(8,128)S(1)}, f32[8,4608]{1,0:T(8,128)}, u32[]{:S(2)}) copy-start(f32[8,4608]{1,0:T(8,128)} %param.7) | copy-start | bytes 442372
  0.6 2.0 %collective-permute-start = (bf16[32,4608]{1,0:T(8,128)(2,1)}, bf16[32,4608]{1,0:T(8,128)(2,1)S(1)}, u32[]{:S(2)}, u32[]{:S(2)}) collective-permute-start(bf16[32,4608]{1,0:T(8,128)(2,1)} %bitcast.8), channel_id=1, source_target_pairs={{0,1},{1,0},{2,3},{3,2},{4,5},{5,4},{6,7},{7,6},{8,9},{9,8},{10,11... | collective-permute-start | bytes 884744 | tf_op jit(solution)/shard_map/ppermute | solution.py:81
  2.6 7.6 %collective-permute-start.8 = (bf16[8,2304]{1,0:T(8,128)(2,1)S(1)}, bf16[8,2304]{1,0:T(8,128)(2,1)S(1)}, u32[]{:S(2)}, u32[]{:S(2)}) collective-permute-start(bf16[8,2304]{1,0:T(8,128)(2,1)S(1)} %dynamic-slice_convert_fusion.2), channel_id=1, source_target_pairs={{0,8},{1,9},{2,10},{3,11},{4,12},{5,13},{6,14},{7,15},{8,0},{9,1},... | collective-permute-start | bytes 110600 | tf_op jit(solution)/shard_map/ppermute | solution.py:81
  6.6 5.4 %collective-permute-start.3 = (bf16[32,1152]{1,0:T(8,128)(2,1)S(1)}, bf16[32,1152]{1,0:T(8,128)(2,1)S(1)}, u32[]{:S(2)}, u32[]{:S(2)}) collective-permute-start(bf16[32,1152]{1,0:T(8,128)(2,1)S(1)} %get-tuple-element.16), channel_id=1, source_target_pairs={{0,6},{1,7},{2,4},{3,5},{4,2},{5,3},{6,0},{7,1},{8,14},{9,15},{10,... | collective-permute-start | bytes 221192 | tf_op jit(solution)/shard_map/ppermute | solution.py:81
  9.2 5.1 %collective-permute-start.1 = (bf16[32,1152]{1,0:T(8,128)(2,1)S(1)}, bf16[32,1152]{1,0:T(8,128)(2,1)S(1)}, u32[]{:S(2)}, u32[]{:S(2)}) collective-permute-start(bf16[32,1152]{1,0:T(8,128)(2,1)S(1)} %get-tuple-element.16), channel_id=1, source_target_pairs={{0,2},{1,3},{2,0},{3,1},{4,6},{5,7},{6,4},{7,5},{8,10},{9,11},{10,... | collective-permute-start | bytes 221192 | tf_op jit(solution)/shard_map/ppermute | solution.py:81
  9.7 4.6 %collective-permute-start.2 = (bf16[32,1152]{1,0:T(8,128)(2,1)S(1)}, bf16[32,1152]{1,0:T(8,128)(2,1)S(1)}, u32[]{:S(2)}, u32[]{:S(2)}) collective-permute-start(bf16[32,1152]{1,0:T(8,128)(2,1)S(1)} %get-tuple-element.15), channel_id=1, source_target_pairs={{0,4},{1,5},{2,6},{3,7},{4,0},{5,1},{6,2},{7,3},{8,12},{9,13},{10,... | collective-permute-start | bytes 221192 | tf_op jit(solution)/shard_map/ppermute | solution.py:81
  10.2 4.9 %collective-permute-start.9 = (bf16[16,2304]{1,0:T(8,128)(2,1)S(1)}, bf16[16,2304]{1,0:T(8,128)(2,1)S(1)}, u32[]{:S(2)}, u32[]{:S(2)}) collective-permute-start(bf16[16,2304]{1,0:T(8,128)(2,1)S(1)} %pad_maximum_fusion.2), channel_id=1, source_target_pairs={{0,4},{1,5},{2,6},{3,7},{4,0},{5,1},{6,2},{7,3},{8,12},{9,13},{10,... | collective-permute-start | bytes 221192 | tf_op jit(solution)/shard_map/ppermute | solution.py:81
  14.4 5.3 %collective-permute-start.4 = (bf16[32,1152]{1,0:T(8,128)(2,1)S(1)}, bf16[32,1152]{1,0:T(8,128)(2,1)S(1)}, u32[]{:S(2)}, u32[]{:S(2)}) collective-permute-start(bf16[32,1152]{1,0:T(8,128)(2,1)S(1)} %fusion.3), channel_id=1, source_target_pairs={{0,8},{1,9},{2,10},{3,11},{4,12},{5,13},{6,14},{7,15},{8,0},{9,1},... | collective-permute-start | bytes 221192 | tf_op jit(solution)/shard_map/ppermute | solution.py:81
  15.2 10.9 %collective-permute-start.10 = (bf16[32,2304]{1,0:T(8,128)(2,1)S(1)}, bf16[32,2304]{1,0:T(8,128)(2,1)S(1)}, u32[]{:S(2)}, u32[]{:S(2)}) collective-permute-start(bf16[32,2304]{1,0:T(8,128)(2,1)S(1)} %pad_maximum_fusion.1), channel_id=1, source_target_pairs={{0,1},{1,0},{2,3},{3,2},{4,5},{5,4},{6,7},{7,6},{8,9},{9,8},{10,11... | collective-permute-start | bytes 442376 | tf_op jit(solution)/shard_map/ppermute | solution.py:81
  19.7 2.4 %copy-start.2 = (f32[8,4608]{1,0:T(8,128)S(1)}, f32[8,4608]{1,0:T(8,128)}, u32[]{:S(2)}) copy-start(f32[8,4608]{1,0:T(8,128)} %param.5) | copy-start | bytes 442372
  19.8 2.4 %copy-start.1 = (f32[8,4608]{1,0:T(8,128)S(1)}, f32[8,4608]{1,0:T(8,128)}, u32[]{:S(2)}) copy-start(f32[8,4608]{1,0:T(8,128)} %param.6) | copy-start | bytes 442372
  19.9 3.9 %collective-permute-start.5 = (bf16[8,1408]{1,0:T(8,128)(2,1)S(1)}, bf16[8,1408]{1,0:T(8,128)(2,1)S(1)}, u32[]{:S(2)}, u32[]{:S(2)}) collective-permute-start(bf16[8,1408]{1,0:T(8,128)(2,1)S(1)} %pad_maximum_fusion.3.own_ref), channel_id=1, source_target_pairs={{0,2},{1,3},{2,0},{3,1},{4,6},{5,7},{6,4},{7,5},{8,10},{9,11},{10,... | collective-permute-start | bytes 67592 | tf_op jit(solution)/shard_map/ppermute | solution.py:81
  22.0 1.8 %collective-permute-start.6 = (bf16[8,1408]{1,0:T(8,128)(2,1)S(1)}, bf16[8,1408]{1,0:T(8,128)(2,1)S(1)}, u32[]{:S(2)}, u32[]{:S(2)}) collective-permute-start(bf16[8,1408]{1,0:T(8,128)(2,1)S(1)} %pad_maximum_fusion.3.own_ref), channel_id=1, source_target_pairs={{0,1},{1,0},{2,3},{3,2},{4,5},{5,4},{6,7},{7,6},{8,9},{9,8},{10,11... | collective-permute-start | bytes 67592 | tf_op jit(solution)/shard_map/ppermute | solution.py:81
  22.0 3.2 %collective-permute-start.7 = (bf16[8,1408]{1,0:T(8,128)(2,1)S(1)}, bf16[8,1408]{1,0:T(8,128)(2,1)S(1)}, u32[]{:S(2)}, u32[]{:S(2)}) collective-permute-start(bf16[8,1408]{1,0:T(8,128)(2,1)S(1)} %pad_maximum_fusion.3.own_ref), channel_id=1, source_target_pairs={{0,3},{1,2},{2,1},{3,0},{4,7},{5,6},{6,5},{7,4},{8,11},{9,10},{10,... | collective-permute-start | bytes 67592 | tf_op jit(solution)/shard_map/ppermute | solution.py:81

commit v4 on v3

--- a/solution.py
+++ b/solution.py
@@ -42,22 +42,29 @@
     sq = total * total
     sq = jnp.pad(sq, ((0, 0), (0, -sq.shape[1] % LANES)))
     sq = sum(sq[:, k : k + LANES] for k in range(0, sq.shape[1], LANES))
-    return jnp.sum(sq.reshape(-1, rows, LANES), axis=0)
+    return jnp.sum(sq.reshape(-1, rows // 2, LANES), axis=0)
 
 
-def finish(entries, at_ref, own_ref, rep_ref, sub_ref, both_ref, base_m_ref, base_p_ref, np_ref, nm_ref, np_buf, nm_buf, sems):
-    width = own_ref.shape[1] - 2 * LANES
+def finish(entries, at_ref, own_ref, rep_ref, sub_ref, both_ref, base_m_ref, base_p_ref, prev_ref, prev_other_ref,
+           np_ref, nm_ref, prev_out_ref, np_buf, nm_buf, sems):
+    width = own_ref.shape[1] - LANES
+    half = prev_ref.shape[1]
+    at = at_ref[0]
+    copies = []
+    for k, ref in enumerate((prev_ref, prev_other_ref)):
+        cols = pl.ds(pl.multiple_of(((at // 2) ^ k) * half, LANES), half)
+        copies.append(pltpu.make_async_copy(ref, prev_out_ref.at[:, cols], sems.at[8 + k]))
+        copies[-1].start()
 
     def squares(ref):
-        return ref[:, width : width + LANES].astype(F32) + ref[:, width + LANES :].astype(F32)
+        both = ref[:, width:].astype(F32)
+        return both[: both.shape[0] // 2] + both[both.shape[0] // 2 :]
 
     total = (squares(own_ref) + squares(rep_ref)) + (squares(sub_ref) + squares(both_ref))
     total = jnp.sum(jnp.sum(total, axis=0, keepdims=True), axis=1, keepdims=True)
     clip_factor = jnp.minimum(
         1.0, jnp.sqrt(jnp.full((1, 1), entries, F32)) / jnp.sqrt(total + 1e-06)
     )
-    at = at_ref[0]
-    copies = []
     for k, ref in enumerate((own_ref, rep_ref, sub_ref, both_ref)):
         cols = pl.ds(pl.multiple_of((at ^ k) * width, LANES), width)
         scaled = clip_factor * ref[:, :width].astype(F32)
@@ -113,13 +120,15 @@
 
         def pack(own, squares):
             high = lax.reduce_precision(squares, 8, 7)
-            return jnp.concatenate([own, high.astype(BF16), (squares - high).astype(BF16)], axis=1)
+            both = jnp.concatenate([high, squares - high], axis=0).astype(BF16)
+            return jnp.concatenate([own, both], axis=1)
 
         for bit in reversed(bits_of(n_rep)[1:]):
             packed = swap(pack(own, squares), rep=bit)
             n = own.shape[1]
             own = joined(own, packed[:, :n], "rep", bit, 1)
-            squares = squares + packed[:, n : n + LANES].astype(F32) + packed[:, n + LANES :].astype(F32)
+            both = packed[:, n:].astype(F32)
+            squares = squares + both[: rows // 2] + both[rows // 2 :]
         packed = pack(own, squares)
         from_rep = swap(packed, rep=1)
         from_sub = swap(packed, sub=1)
@@ -130,25 +139,24 @@
         order = [sum(((b >> k) & 1) * (n_blk >> (k + 1)) for k in range(n_blk.bit_length() - 1)) for b in range(n_blk)]
         prev = jnp.concatenate([prev[o * rows : (o + 1) * rows] for o in order], axis=0)
         prev_other = swap(prev, sub=1)
-        prev = joined(prev, prev_other, "sub", 1, 1)
 
         base_m = momentum_coef * momentum
         base_p = params - outer_rate * momentum_coef * base_m
         at = (2 * lax.axis_index("sub") + mine("rep", 1)).reshape(1)
         vmem, hbm = pl.BlockSpec(memory_space=pltpu.VMEM), pl.BlockSpec(memory_space=pl.ANY)
         out = jax.ShapeDtypeStruct(params.shape, F32)
-        new_params, new_momentum = pl.pallas_call(
+        new_params, new_momentum, prev = pl.pallas_call(
             functools.partial(finish, float(entries)),
-            out_shape=(out, out),
-            in_specs=[pl.BlockSpec(memory_space=pltpu.SMEM)] + [vmem] * 6,
-            out_specs=(hbm, hbm),
+            out_shape=(out, out, jax.ShapeDtypeStruct((prev.shape[0], width), BF16)),
+            in_specs=[pl.BlockSpec(memory_space=pltpu.SMEM)] + [vmem] * 8,
+            out_specs=(hbm, hbm, hbm),
             scratch_shapes=[
                 pltpu.VMEM(params.shape, F32),
                 pltpu.VMEM(params.shape, F32),
-                pltpu.SemaphoreType.DMA((8,)),
+                pltpu.SemaphoreType.DMA((10,)),
             ],
             compiler_params=pltpu.CompilerParams(vmem_limit_bytes=4 << 20),
-        )(at, packed, from_rep, from_sub, from_both, base_m, base_p)
+        )(at, packed, from_rep, from_sub, from_both, base_m, base_p, prev, prev_other)
         return (new_params, new_momentum, prev)
 
     return per_device

time: 27 us -> 26.9 us (level)
  other arithmetic: 1.03 us -> 0.27 us
  waiting for transfers between devices: 10.5 us -> 11.2 us
    concatenate x2 -> x1, other arithmetic: 0.74 us -> 0.01 us  [joined(): jnp.concatenate([jnp.where(upper, other, own), jnp.where(upper, own, othe...]
    ppermute x11, waiting for transfers between devices: 10.5 us -> 11.2 us  [swap(): return lax.ppermute(value, GROUP, pairs)]
  transfers between devices with their start and end apart: 11 -> 11, of which waited for: 7 -> 6; matrix products, arithmetic and copies ran while one was open for 5% -> 5% of each run, Pallas kernels for 3% -> 0%
where the time goes in v4:
time: 26.9 us; the launch traced here: 26.8 us
  starting transfers between devices  12.6 us (47%)
  waiting for transfers between devices  11.2 us (42%)
  local copies, waits for them, and re-layouts  1.01 us (4%)
  Pallas kernels  0.91 us (3%)
  between operations  0.77 us (3%)
  other arithmetic  0.27 us (1%)
    ppermute x11, starting transfers between devices, swap(): return lax.ppermute(value, GROUP, pairs)  12.6 us
    ppermute x11, waiting for transfers between devices, swap(): return lax.ppermute(value, GROUP, pairs)  11.2 us
    dynamic_slice x1, local copies, waits for them, and re-layouts, halves(): keep = lax.dynamic_slice_in_dim(value, at, half, 1)  0.92 us
    pallas_call x1, Pallas kernels, step(): pl.pallas_call(functools.partial(finish, float(entries)), out_shape=(out,...  0.91 us
  transfers between devices with their start and end apart: 11, of which 6 were waited for; matrix products, arithmetic and copies ran while one was open for 5% of the time, Pallas kernels for 0%

profile of v4, /device:TPU:0, one launch (start us, length us, event | category | flops | bytes accessed | tf_op | source)
XLA Modules:
  0.0 26.8 jit_solution(8568266288375861192)
XLA Ops:
  0.6 0.0 copy-start
  0.6 0.6 %collective-permute-start = (bf16[32,4608]{1,0:T(8,128)(2,1)}, bf16[32,4608]{1,0:T(8,128)(2,1)S(1)}, u32[]{:S(2)}, u32[]{:S(2)}) collective-permute-start(bf16[32,4608]{1,0:T(8,128)(2,1)} %bitcast.5), channel_id=1, source_target_pairs={{0,1},{1,0},{2,3},{3,2},{4,5},{5,4},{6,7},{7,6},{8,9},{9,8},{10,11... | collective-permute-start | bytes 884744 | tf_op jit(solution)/shard_map/ppermute | solution.py:88
  1.2 0.9 %dynamic-slice_bitcast_fusion = bf16[32,2304]{1,0:T(8,128)(2,1)S(1)} fusion(bf16[1,32,4608]{2,1,0:T(8,128)(2,1)} %param.4, s32[]{:T(128)S(6)} %select_n.49), kind=kLoop, calls=%fused_computation.6 | loop fusion | bytes 294916 | tf_op jit(solution)/shard_map/dynamic_slice | solution.py:29
  2.1 0.0 copy-done
  2.2 0.5 %collective-permute-done = bf16[32,4608]{1,0:T(8,128)(2,1)S(1)} collective-permute-done((bf16[32,4608]{1,0:T(8,128)(2,1)}, bf16[32,4608]{1,0:T(8,128)(2,1)S(1)}, u32[]{:S(2)}, u32[]{:S(2)}) %collective-permute-start) | collective-permute-done | bytes 294944 | tf_op jit(solution)/shard_map/ppermute | solution.py:88
  2.6 3.9 %collective-permute-start.8 = (bf16[8,2304]{1,0:T(8,128)(2,1)S(1)}, bf16[8,2304]{1,0:T(8,128)(2,1)S(1)}, u32[]{:S(2)}, u32[]{:S(2)}) collective-permute-start(bf16[8,2304]{1,0:T(8,128)(2,1)S(1)} %dynamic-slice_convert_fusion.2), channel_id=1, source_target_pairs={{0,8},{1,9},{2,10},{3,11},{4,12},{5,13},{6,14},{7,15},{8,0},{9,1},... | collective-permute-start | bytes 110600 | tf_op jit(solution)/shard_map/ppermute | solution.py:88
  6.6 2.6 %collective-permute-start.3 = (bf16[32,1152]{1,0:T(8,128)(2,1)S(1)}, bf16[32,1152]{1,0:T(8,128)(2,1)S(1)}, u32[]{:S(2)}, u32[]{:S(2)}) collective-permute-start(bf16[32,1152]{1,0:T(8,128)(2,1)S(1)} %get-tuple-element.10), channel_id=1, source_target_pairs={{0,6},{1,7},{2,4},{3,5},{4,2},{5,3},{6,0},{7,1},{8,14},{9,15},{10,... | collective-permute-start | bytes 221192 | tf_op jit(solution)/shard_map/ppermute | solution.py:88
  9.2 0.5 %collective-permute-start.1 = (bf16[32,1152]{1,0:T(8,128)(2,1)S(1)}, bf16[32,1152]{1,0:T(8,128)(2,1)S(1)}, u32[]{:S(2)}, u32[]{:S(2)}) collective-permute-start(bf16[32,1152]{1,0:T(8,128)(2,1)S(1)} %get-tuple-element.10), channel_id=1, source_target_pairs={{0,2},{1,3},{2,0},{3,1},{4,6},{5,7},{6,4},{7,5},{8,10},{9,11},{10,... | collective-permute-start | bytes 221192 | tf_op jit(solution)/shard_map/ppermute | solution.py:88
  9.7 0.4 %collective-permute-start.2 = (bf16[32,1152]{1,0:T(8,128)(2,1)S(1)}, bf16[32,1152]{1,0:T(8,128)(2,1)S(1)}, u32[]{:S(2)}, u32[]{:S(2)}) collective-permute-start(bf16[32,1152]{1,0:T(8,128)(2,1)S(1)} %get-tuple-element.9), channel_id=1, source_target_pairs={{0,4},{1,5},{2,6},{3,7},{4,0},{5,1},{6,2},{7,3},{8,12},{9,13},{10,... | collective-permute-start | bytes 221192 | tf_op jit(solution)/shard_map/ppermute | solution.py:88
  10.2 0.0 collective-permute-done.8
  10.2 1.6 %collective-permute-start.9 = (bf16[16,2304]{1,0:T(8,128)(2,1)S(1)}, bf16[16,2304]{1,0:T(8,128)(2,1)S(1)}, u32[]{:S(2)}, u32[]{:S(2)}) collective-permute-start(bf16[16,2304]{1,0:T(8,128)(2,1)S(1)} %pad_maximum_fusion.1), channel_id=1, source_target_pairs={{0,4},{1,5},{2,6},{3,7},{4,0},{5,1},{6,2},{7,3},{8,12},{9,13},{10,... | collective-permute-start | bytes 221192 | tf_op jit(solution)/shard_map/ppermute | solution.py:88
  11.9 2.5 %collective-permute-done.2 = bf16[32,1152]{1,0:T(8,128)(2,1)S(1)} collective-permute-done((bf16[32,1152]{1,0:T(8,128)(2,1)S(1)}, bf16[32,1152]{1,0:T(8,128)(2,1)S(1)}, u32[]{:S(2)}, u32[]{:S(2)}) %collective-permute-start.2) | collective-permute-done | bytes 73760 | tf_op jit(solution)/shard_map/ppermute | solution.py:88
  14.4 0.0 collective-permute-done.3
  14.4 0.0 collective-permute-done.1
  14.4 0.6 %collective-permute-start.4 = (bf16[32,1152]{1,0:T(8,128)(2,1)S(1)}, bf16[32,1152]{1,0:T(8,128)(2,1)S(1)}, u32[]{:S(2)}, u32[]{:S(2)}) collective-permute-start(bf16[32,1152]{1,0:T(8,128)(2,1)S(1)} %fusion.1), channel_id=1, source_target_pairs={{0,8},{1,9},{2,10},{3,11},{4,12},{5,13},{6,14},{7,15},{8,0},{9,1},... | collective-permute-start | bytes 221192 | tf_op jit(solution)/shard_map/ppermute | solution.py:88
  15.0 0.1 collective-permute-done.9
  15.2 0.1 collective-permute-start.10
  15.3 4.4 %collective-permute-done.4 = bf16[32,1152]{1,0:T(8,128)(2,1)S(1)} collective-permute-done((bf16[32,1152]{1,0:T(8,128)(2,1)S(1)}, bf16[32,1152]{1,0:T(8,128)(2,1)S(1)}, u32[]{:S(2)}, u32[]{:S(2)}) %collective-permute-start.4) | collective-permute-done | bytes 73760 | tf_op jit(solution)/shard_map/ppermute | solution.py:88
  19.7 0.0 copy-start.2
  19.7 0.1 fusion.2
  19.8 0.0 copy-start.1
  19.9 0.1 collective-permute-start.7
  20.0 2.1 %collective-permute-start.6 = (bf16[8,1280]{1,0:T(8,128)(2,1)S(1)}, bf16[8,1280]{1,0:T(8,128)(2,1)S(1)}, u32[]{:S(2)}, u32[]{:S(2)}) collective-permute-start(bf16[8,1280]{1,0:T(8,128)(2,1)S(1)} %maximum_maximum_fusion.own_ref), channel_id=1, source_target_pairs={{0,1},{1,0},{2,3},{3,2},{4,5},{5,4},{6,7},{7,6},{8,9},{9,8},{10,11... | collective-permute-start | bytes 61448 | tf_op jit(solution)/shard_map/ppermute | solution.py:88
  22.1 0.0 collective-permute-start.5
  22.1 0.0 copy-done.2
  22.1 0.0 copy-done.1
  22.2 1.0 %collective-permute-done.7.both_ref = bf16[8,1280]{1,0:T(8,128)(2,1)S(1)} collective-permute-done((bf16[8,1280]{1,0:T(8,128)(2,1)S(1)}, bf16[8,1280]{1,0:T(8,128)(2,1)S(1)}, u32[]{:S(2)}, u32[]{:S(2)}) %collective-permute-start.7) | collective-permute-done | bytes 20512 | tf_op jit(solution)/shard_map/ppermute | solution.py:88
  23.2 0.0 collective-permute-done.6.sub_ref
  23.2 2.7 %collective-permute-done.5.rep_ref = bf16[8,1280]{1,0:T(8,128)(2,1)S(1)} collective-permute-done((bf16[8,1280]{1,0:T(8,128)(2,1)S(1)}, bf16[8,1280]{1,0:T(8,128)(2,1)S(1)}, u32[]{:S(2)}, u32[]{:S(2)}) %collective-permute-start.5) | collective-permute-done | bytes 20512 | tf_op jit(solution)/shard_map/ppermute | solution.py:88
  25.9 0.0 collective-permute-done.10.prev_other_ref
  25.9 0.9 %shard_map.67 = (f32[8,4608]{1,0:T(8,128)}, f32[8,4608]{1,0:T(8,128)}, bf16[32,4608]{1,0:T(8,128)(2,1)}) custom-call(s32[1]{0:T(128)} %bitcast.at_ref, bf16[8,1280]{1,0:T(8,128)(2,1)S(1)} %maximum_maximum_fusion.own_ref, bf16[8,1280]{1,0:T(8,128)(2,1)S(1)} %collective-permute-done.5.rep_ref, bf16[8,1280]{1,0:T(8,128)(2,1)S(1)} %collective-permute-done.6.sub_ref, ...), custom_call_target="tpu_custom_call" | custom-call | tf_op jit(solution)/shard_map/pallas_call | solution.py:148
  (15 shorter events, 0.3 us)
Async XLA Ops:
  0.6 1.5 %copy-start = (f32[8,4608]{1,0:T(8,128)S(1)}, f32[8,4608]{1,0:T(8,128)}, u32[]{:S(2)}) copy-start(f32[8,4608]{1,0:T(8,128)} %param.7) | copy-start | bytes 442372
  0.6 2.0 %collective-permute-start = (bf16[32,4608]{1,0:T(8,128)(2,1)}, bf16[32,4608]{1,0:T(8,128)(2,1)S(1)}, u32[]{:S(2)}, u32[]{:S(2)}) collective-permute-start(bf16[32,4608]{1,0:T(8,128)(2,1)} %bitcast.5), channel_id=1, source_target_pairs={{0,1},{1,0},{2,3},{3,2},{4,5},{5,4},{6,7},{7,6},{8,9},{9,8},{10,11... | collective-permute-start | bytes 884744 | tf_op jit(solution)/shard_map/ppermute | solution.py:88
  2.6 7.6 %collective-permute-start.8 = (bf16[8,2304]{1,0:T(8,128)(2,1)S(1)}, bf16[8,2304]{1,0:T(8,128)(2,1)S(1)}, u32[]{:S(2)}, u32[]{:S(2)}) collective-permute-start(bf16[8,2304]{1,0:T(8,128)(2,1)S(1)} %dynamic-slice_convert_fusion.2), channel_id=1, source_target_pairs={{0,8},{1,9},{2,10},{3,11},{4,12},{5,13},{6,14},{7,15},{8,0},{9,1},... | collective-permute-start | bytes 110600 | tf_op jit(solution)/shard_map/ppermute | solution.py:88
  6.6 7.7 %collective-permute-start.3 = (bf16[32,1152]{1,0:T(8,128)(2,1)S(1)}, bf16[32,1152]{1,0:T(8,128)(2,1)S(1)}, u32[]{:S(2)}, u32[]{:S(2)}) collective-permute-start(bf16[32,1152]{1,0:T(8,128)(2,1)S(1)} %get-tuple-element.10), channel_id=1, source_target_pairs={{0,6},{1,7},{2,4},{3,5},{4,2},{5,3},{6,0},{7,1},{8,14},{9,15},{10,... | collective-permute-start | bytes 221192 | tf_op jit(solution)/shard_map/ppermute | solution.py:88
  9.2 5.2 %collective-permute-start.1 = (bf16[32,1152]{1,0:T(8,128)(2,1)S(1)}, bf16[32,1152]{1,0:T(8,128)(2,1)S(1)}, u32[]{:S(2)}, u32[]{:S(2)}) collective-permute-start(bf16[32,1152]{1,0:T(8,128)(2,1)S(1)} %get-tuple-element.10), channel_id=1, source_target_pairs={{0,2},{1,3},{2,0},{3,1},{4,6},{5,7},{6,4},{7,5},{8,10},{9,11},{10,... | collective-permute-start | bytes 221192 | tf_op jit(solution)/shard_map/ppermute | solution.py:88
  9.7 4.6 %collective-permute-start.2 = (bf16[32,1152]{1,0:T(8,128)(2,1)S(1)}, bf16[32,1152]{1,0:T(8,128)(2,1)S(1)}, u32[]{:S(2)}, u32[]{:S(2)}) collective-permute-start(bf16[32,1152]{1,0:T(8,128)(2,1)S(1)} %get-tuple-element.9), channel_id=1, source_target_pairs={{0,4},{1,5},{2,6},{3,7},{4,0},{5,1},{6,2},{7,3},{8,12},{9,13},{10,... | collective-permute-start | bytes 221192 | tf_op jit(solution)/shard_map/ppermute | solution.py:88
  10.2 4.9 %collective-permute-start.9 = (bf16[16,2304]{1,0:T(8,128)(2,1)S(1)}, bf16[16,2304]{1,0:T(8,128)(2,1)S(1)}, u32[]{:S(2)}, u32[]{:S(2)}) collective-permute-start(bf16[16,2304]{1,0:T(8,128)(2,1)S(1)} %pad_maximum_fusion.1), channel_id=1, source_target_pairs={{0,4},{1,5},{2,6},{3,7},{4,0},{5,1},{6,2},{7,3},{8,12},{9,13},{10,... | collective-permute-start | bytes 221192 | tf_op jit(solution)/shard_map/ppermute | solution.py:88
  14.4 5.3 %collective-permute-start.4 = (bf16[32,1152]{1,0:T(8,128)(2,1)S(1)}, bf16[32,1152]{1,0:T(8,128)(2,1)S(1)}, u32[]{:S(2)}, u32[]{:S(2)}) collective-permute-start(bf16[32,1152]{1,0:T(8,128)(2,1)S(1)} %fusion.1), channel_id=1, source_target_pairs={{0,8},{1,9},{2,10},{3,11},{4,12},{5,13},{6,14},{7,15},{8,0},{9,1},... | collective-permute-start | bytes 221192 | tf_op jit(solution)/shard_map/ppermute | solution.py:88
  15.2 10.7 %collective-permute-start.10 = (bf16[32,2304]{1,0:T(8,128)(2,1)S(1)}, bf16[32,2304]{1,0:T(8,128)(2,1)S(1)}, u32[]{:S(2)}, u32[]{:S(2)}) collective-permute-start(bf16[32,2304]{1,0:T(8,128)(2,1)S(1)} %pad_maximum_fusion.prev_ref), channel_id=1, source_target_pairs={{0,1},{1,0},{2,3},{3,2},{4,5},{5,4},{6,7},{7,6},{8,9},{9,8},{10,11... | collective-permute-start | bytes 442376 | tf_op jit(solution)/shard_map/ppermute | solution.py:88
  19.7 2.4 %copy-start.2 = (f32[8,4608]{1,0:T(8,128)S(1)}, f32[8,4608]{1,0:T(8,128)}, u32[]{:S(2)}) copy-start(f32[8,4608]{1,0:T(8,128)} %param.5) | copy-start | bytes 442372
  19.8 2.3 %copy-start.1 = (f32[8,4608]{1,0:T(8,128)S(1)}, f32[8,4608]{1,0:T(8,128)}, u32[]{:S(2)}) copy-start(f32[8,4608]{1,0:T(8,128)} %param.6) | copy-start | bytes 442372
  19.9 3.3 %collective-permute-start.7 = (bf16[8,1280]{1,0:T(8,128)(2,1)S(1)}, bf16[8,1280]{1,0:T(8,128)(2,1)S(1)}, u32[]{:S(2)}, u32[]{:S(2)}) collective-permute-start(bf16[8,1280]{1,0:T(8,128)(2,1)S(1)} %maximum_maximum_fusion.own_ref), channel_id=1, source_target_pairs={{0,3},{1,2},{2,1},{3,0},{4,7},{5,6},{6,5},{7,4},{8,11},{9,10},{10,... | collective-permute-start | bytes 61448 | tf_op jit(solution)/shard_map/ppermute | solution.py:88
  20.0 3.2 %collective-permute-start.6 = (bf16[8,1280]{1,0:T(8,128)(2,1)S(1)}, bf16[8,1280]{1,0:T(8,128)(2,1)S(1)}, u32[]{:S(2)}, u32[]{:S(2)}) collective-permute-start(bf16[8,1280]{1,0:T(8,128)(2,1)S(1)} %maximum_maximum_fusion.own_ref), channel_id=1, source_target_pairs={{0,1},{1,0},{2,3},{3,2},{4,5},{5,4},{6,7},{7,6},{8,9},{9,8},{10,11... | collective-permute-start | bytes 61448 | tf_op jit(solution)/shard_map/ppermute | solution.py:88
  22.1 3.8 %collective-permute-start.5 = (bf16[8,1280]{1,0:T(8,128)(2,1)S(1)}, bf16[8,1280]{1,0:T(8,128)(2,1)S(1)}, u32[]{:S(2)}, u32[]{:S(2)}) collective-permute-start(bf16[8,1280]{1,0:T(8,128)(2,1)S(1)} %maximum_maximum_fusion.own_ref), channel_id=1, source_target_pairs={{0,2},{1,3},{2,0},{3,1},{4,6},{5,7},{6,4},{7,5},{8,10},{9,11},{10,... | collective-permute-start | bytes 61448 | tf_op jit(solution)/shard_map/ppermute | solution.py:88
